TPU v7x, 128 devices: a whole 4x4x4 slice. The times are simulated.
128 devices in a mesh: problem: 1, samp: 2 (over core), feat: 64 (over z, y, x).
Axes of the slice: x: 4, y: 4, z: 4, core: 2. Of those that a mesh axis runs over, the one named last changes fastest.
Arguments:
- design: bfloat16 [4096, 131072], P(('problem', 'samp'), 'feat')
- targets: float32 [4096, 128], P(('problem', 'samp'))
- coef_init: float32 [131072, 128], P(('problem', 'feat'))
- step_sizes: float32 [131072], P(('problem', 'feat'))
- ridge_weights: float32 [128], P('problem')
Outputs:
- output 1: float32 [131072, 128], P(('problem', 'feat'))
- output 2: float32 [4096, 128], P(('problem', 'samp'))
All inputs are finite; a program needn't handle non-finite values.
Results may differ from a plain program's by a relative error of at most 0.00658185.
Values are sent between devices in bfloat16 or wider.
A program may use at most 1 GiB of HBM per device.

v0:
```python
import jax
import jax.numpy as jnp
from jax import lax
from jax.sharding import PartitionSpec as P

SWEEPS = 4
STEP_WEIGHT = 0.5


def solution(mesh):
    samp_size = mesh.shape["samp"]
    design_spec = P(("problem", "samp"), "feat")
    rows_spec = P(("problem", "samp"), None)
    coef_spec = P(("problem", "feat"), None)
    step_spec = P(("problem", "feat"))
    ridge_spec = P("problem")

    def local_sweeps(design, targets, coef_init, step_sizes, ridge_weights):
        total_rows = design.shape[0] * samp_size
        step_col = step_sizes[:, None]
        ridge_row = ridge_weights[None, :]

        def block_product(weights):
            product = jnp.dot(design, weights.astype(jnp.bfloat16), preferred_element_type=jnp.float32)
            return product.astype(jnp.bfloat16).astype(jnp.float32)

        resid_cur = targets - lax.psum(block_product(coef_init), "feat")
        coef_cur = coef_init
        for sweep_index in range(SWEEPS):
            part_grad = lax.dot_general(design, resid_cur.astype(jnp.bfloat16), (((0,), (0,)), ((), ())), preferred_element_type=jnp.float32)
            gradient = lax.psum(part_grad, "samp") / total_rows
            step_delta = step_col * (gradient - ridge_row * coef_cur)
            coef_cur = coef_cur + STEP_WEIGHT * step_delta
            resid_cur = resid_cur - STEP_WEIGHT * lax.psum(block_product(step_delta), "feat")
        return coef_cur, resid_cur

    return jax.shard_map(local_sweeps, mesh=mesh, in_specs=(design_spec, rows_spec, coef_spec, step_spec, ridge_spec), out_specs=(coef_spec, rows_spec), check_vma=False)
```

profile of v0, /device:TPU:0, one launch (start us, length us, event | category | flops | bytes accessed | tf_op | source)
XLA Modules:
  0.0 840.6 jit_solution(6959150836179534169)
XLA Ops:
  7.2 0.0 copy-start.3
  7.2 0.0 all-reduce.10.cloned.1.call-start
  7.2 7.0 fusion.8
  14.2 0.0 copy-start
  14.2 0.0 copy-start.4
  14.2 0.0 copy-start.5
  14.2 0.0 all-reduce.10.cloned.1.call-update
  14.3 0.0 all-reduce.12.cloned.1.call-start
  14.3 134.0 %all-reduce.10.cloned.1.call-done = f32[2048,128]{1,0:T(8,128)} async-done(((f32[2048,128]{1,0:T(8,128)}), f32[2048,128]{1,0:T(8,128)}) %all-reduce.10.cloned.1.call-update) | async-done | bytes 1048592 | tf_op jit(solution)/shard_map/psum | solution.py:27
  148.3 0.0 copy-done.3
  148.3 1.3 sub.27
  149.7 7.7 convolution_bitcast_fusion.3
  157.4 0.0 all-reduce.12.cloned.1.call-update
  157.4 0.0 all-reduce.14.cloned.1.call-start
  157.5 22.1 %all-reduce.12.cloned.1.call-done = f32[2048,128]{1,0:T(8,128)} async-done(((f32[2048,128]{1,0:T(8,128)}), f32[2048,128]{1,0:T(8,128)}) %all-reduce.12.cloned.1.call-update) | async-done | bytes 1048592 | tf_op jit(solution)/shard_map/psum | solution.py:31
  179.6 0.0 copy-done
  179.6 0.0 copy-done.4
  179.6 0.0 copy-done.5
  179.6 7.0 fusion.7
  186.6 0.0 copy-start.1
  186.6 0.0 all-reduce.14.cloned.1.call-update
  186.6 0.0 all-reduce.16.cloned.1.call-start
  186.7 132.8 %all-reduce.14.cloned.1.call-done = f32[2048,128]{1,0:T(8,128)} async-done(((f32[2048,128]{1,0:T(8,128)}), f32[2048,128]{1,0:T(8,128)}) %all-reduce.14.cloned.1.call-update) | async-done | bytes 1048592 | tf_op jit(solution)/shard_map/psum | solution.py:34
  319.5 8.1 convolution_bitcast_fusion.2
  327.6 0.0 all-reduce.16.cloned.1.call-update
  327.6 0.2 all-reduce.18.cloned.1.call-start
  327.8 21.9 %all-reduce.16.cloned.1.call-done = f32[2048,128]{1,0:T(8,128)} async-done(((f32[2048,128]{1,0:T(8,128)}), f32[2048,128]{1,0:T(8,128)}) %all-reduce.16.cloned.1.call-update) | async-done | bytes 1048592 | tf_op jit(solution)/shard_map/psum | solution.py:31
  349.7 0.0 copy-done.1
  349.8 7.0 fusion.5
  356.8 0.0 all-reduce.18.cloned.1.call-update
  356.8 0.0 all-reduce.20.cloned.1.call-start
  356.9 132.8 %all-reduce.18.cloned.1.call-done = f32[2048,128]{1,0:T(8,128)} async-done(((f32[2048,128]{1,0:T(8,128)}), f32[2048,128]{1,0:T(8,128)}) %all-reduce.18.cloned.1.call-update) | async-done | bytes 1048592 | tf_op jit(solution)/shard_map/psum | solution.py:34
  489.7 1.7 multiply_subtract_fusion.2
  491.4 7.7 convolution_bitcast_fusion.1
  499.1 0.0 all-reduce.20.cloned.1.call-update
  499.1 0.0 all-reduce.22.cloned.1.call-start
  499.2 2.0 multiply_add_fusion.2
  501.2 20.1 %all-reduce.20.cloned.1.call-done = f32[2048,128]{1,0:T(8,128)} async-done(((f32[2048,128]{1,0:T(8,128)}), f32[2048,128]{1,0:T(8,128)}) %all-reduce.20.cloned.1.call-update) | async-done | bytes 1048592 | tf_op jit(solution)/shard_map/psum | solution.py:31
  521.3 7.0 fusion.3
  528.3 0.0 copy-start.2
  528.3 0.0 all-reduce.22.cloned.1.call-update
  528.3 0.3 all-reduce.24.cloned.1.call-start
  528.6 132.6 %all-reduce.22.cloned.1.call-done = f32[2048,128]{1,0:T(8,128)} async-done(((f32[2048,128]{1,0:T(8,128)}), f32[2048,128]{1,0:T(8,128)}) %all-reduce.22.cloned.1.call-update) | async-done | bytes 1048592 | tf_op jit(solution)/shard_map/psum | solution.py:34
  661.2 8.1 convolution_bitcast_fusion
  669.3 0.0 all-reduce.24.cloned.1.call-update
  669.3 0.0 all-reduce.26.cloned.1.call-start
  669.3 22.1 %all-reduce.24.cloned.1.call-done = f32[2048,128]{1,0:T(8,128)} async-done(((f32[2048,128]{1,0:T(8,128)}), f32[2048,128]{1,0:T(8,128)}) %all-reduce.24.cloned.1.call-update) | async-done | bytes 1048592 | tf_op jit(solution)/shard_map/psum | solution.py:31
  691.5 0.0 copy-done.2
  691.5 7.0 fusion.1
  698.5 0.0 all-reduce.26.cloned.1.call-update
  698.5 2.6 multiply_add_fusion
  701.2 130.2 %all-reduce.26.cloned.1.call-done = f32[2048,128]{1,0:T(8,128)} async-done(((f32[2048,128]{1,0:T(8,128)}), f32[2048,128]{1,0:T(8,128)}) %all-reduce.26.cloned.1.call-update) | async-done | bytes 1048592 | tf_op jit(solution)/shard_map/psum | solution.py:34
  831.4 2.6 multiply_subtract_fusion
Async XLA Ops:
  7.2 141.2 %copy-start.3 = (f32[2048,128]{1,0:T(8,128)S(1)}, f32[2048,128]{1,0:T(8,128)}, u32[]{:S(2)}) copy-start(f32[2048,128]{1,0:T(8,128)} %param.6) | copy-start | bytes 3145732
  7.2 141.1 %all-reduce.10.cloned.1.call-start = ((), (), s32[]{:S(2)}) async-start(), calls=%async_computation | async-start | bytes 2097152 | tf_op jit(solution)/shard_map/psum | solution.py:27
  14.2 165.3 %copy-start = (f32[2048,128]{1,0:T(8,128)S(1)}, f32[2048,128]{1,0:T(8,128)}, u32[]{:S(2)}) copy-start(f32[2048,128]{1,0:T(8,128)} %param.7) | copy-start | bytes 3145732
  14.2 165.3 %copy-start.4 = (f32[2048]{0:T(1024)S(1)}, f32[2048]{0:T(1024)}, u32[]{:S(2)}) copy-start(f32[2048]{0:T(1024)} %param.8) | copy-start | bytes 24580
  14.2 165.3 %copy-start.5 = (f32[128]{0:T(128)S(1)}, f32[128]{0:T(128)}, u32[]{:S(2)}) copy-start(f32[128]{0:T(128)} %param.9) | copy-start | bytes 1540
  14.3 165.3 %all-reduce.12.cloned.1.call-start = ((), (), s32[]{:S(2)}) async-start(), calls=%async_computation.1 | async-start | bytes 2097152 | tf_op jit(solution)/shard_map/psum | solution.py:31
  157.4 162.1 %all-reduce.14.cloned.1.call-start = ((), (), s32[]{:S(2)}) async-start(), calls=%async_computation.2 | async-start | bytes 2097152 | tf_op jit(solution)/shard_map/psum | solution.py:34
  186.6 163.1 %copy-start.1 = (f32[2048,128]{1,0:T(8,128)S(1)}, f32[2048,128]{1,0:T(8,128)}, u32[]{:S(2)}) copy-start(f32[2048,128]{1,0:T(8,128)} %all-reduce.12.cloned.1.call-done) | copy-start | bytes 3145732
  186.6 163.1 %all-reduce.16.cloned.1.call-start = ((), (), s32[]{:S(2)}) async-start(), calls=%async_computation.3 | async-start | bytes 2097152 | tf_op jit(solution)/shard_map/psum | solution.py:31
  327.6 162.1 %all-reduce.18.cloned.1.call-start = ((), (), s32[]{:S(2)}) async-start(), calls=%async_computation.4 | async-start | bytes 2097152 | tf_op jit(solution)/shard_map/psum | solution.py:34
  356.8 164.5 %all-reduce.20.cloned.1.call-start = ((), (), s32[]{:S(2)}) async-start(), calls=%async_computation.5 | async-start | bytes 2097152 | tf_op jit(solution)/shard_map/psum | solution.py:31
  499.1 162.1 %all-reduce.22.cloned.1.call-start = ((), (), s32[]{:S(2)}) async-start(), calls=%async_computation.6 | async-start | bytes 2097152 | tf_op jit(solution)/shard_map/psum | solution.py:34
  528.3 163.1 %copy-start.2 = (f32[2048,128]{1,0:T(8,128)S(1)}, f32[2048,128]{1,0:T(8,128)}, u32[]{:S(2)}) copy-start(f32[2048,128]{1,0:T(8,128)} %all-reduce.20.cloned.1.call-done) | copy-start | bytes 3145732
  528.3 163.1 %all-reduce.24.cloned.1.call-start = ((), (), s32[]{:S(2)}) async-start(), calls=%async_computation.7 | async-start | bytes 2097152 | tf_op jit(solution)/shard_map/psum | solution.py:31
  669.3 162.1 %all-reduce.26.cloned.1.call-start = ((), (), s32[]{:S(2)}) async-start(), calls=%async_computation.8 | async-start | bytes 2097152 | tf_op jit(solution)/shard_map/psum | solution.py:34
Sparse Core Ops, SparseCore 0:
  14.4 133.8 all-reduce.9
  157.5 21.9 all-reduce.11
  186.8 132.6 all-reduce.13
  327.7 21.9 all-reduce.15
  356.9 132.6 all-reduce.17
  499.2 22.0 all-reduce.19
  528.5 132.6 all-reduce.21
  669.4 21.9 all-reduce.23
  698.6 132.6 all-reduce.25
where the time goes:
time: 841 us
  waiting for transfers between devices  749 us (89%)
  matrix products  66.7 us (8%)
  between operations  13.9 us (2%)
  other arithmetic  10.3 us (1%)
    psum x4, waiting for transfers between devices, local_sweeps(): lax.psum(block_product(step_delta), 'feat')  528 us
    psum x1, waiting for transfers between devices, local_sweeps(): resid_cur = targets - lax.psum(block_product(coef_init), 'feat')  134 us
    psum x4, waiting for transfers between devices, local_sweeps(): gradient = lax.psum(part_grad, 'samp') / total_rows  86.3 us
    dot_general x5, matrix products, block_product(): jnp.dot(design, weights.astype(jnp.bfloat16), preferred_element_type=jnp....  35.2 us
    dot_general x4, matrix products, local_sweeps(): lax.dot_general(design, resid_cur.astype(jnp.bfloat16), (((0,), (0,)), ((...  31.6 us
  transfers between devices with their start and end apart: 9, of which 9 were waited for; matrix products, arithmetic and copies ran while one was open for 1% of the time, Pallas kernels for 0%

commit v1 on v0

v1 whole, which is shorter than its diff:
```python
import functools

import jax
import jax.numpy as jnp
from jax import lax
from jax.experimental import pallas as pl
from jax.experimental.pallas import tpu as pltpu
from jax.sharding import PartitionSpec as P

SWEEPS = 4
STEP_WEIGHT = 0.5
FT = 256


def _kernel(side, n_feat, n_samp, x_hbm, y_hbm, w0_hbm, eta_ref, lam_ref, w_out, r_out,
            x_v, w_nat, w_t, sb, u_buf, rs_recv, rb_full, gt, g_recv, rs_res, rf_full, rf_own,
            x_sem, in_sem, rs_ssem, rs_rsem, ag_ssem, ag_rsem, g_ssem, g_rsem, out_sem):
    rows, feats = x_v.shape
    targets = w_nat.shape[1]
    own = rows // n_feat
    per_z = n_feat // side
    zrows = rows // side
    n_ft = feats // FT
    total_rows = rows * n_samp

    me = lax.axis_index("feat")
    core = lax.axis_index("samp")
    mz, my, mx = me // (side * side), (me // side) % side, me % side

    def peer_of(dz, dy, dx):
        return ((mz + dz) % side) * (side * side) + ((my + dy) % side) * side + (mx + dx) % side

    barrier = pltpu.get_barrier_semaphore()
    for d in range(1, n_feat):
        pl.semaphore_signal(barrier, inc=1, device_id={"feat": peer_of(d // (side * side), (d // side) % side, d % side)},
                            device_id_type=pl.DeviceIdType.MESH)
    pl.semaphore_signal(barrier, inc=1, device_id={"samp": 1 - core}, device_id_type=pl.DeviceIdType.MESH)

    w_load = pltpu.make_async_copy(w0_hbm, w_nat, in_sem.at[0])
    w_load.start()

    def x_load(k):
        z_rows = pl.ds(pl.multiple_of(((mz + k + 1) % side) * zrows, zrows), zrows)
        return pltpu.make_async_copy(x_hbm.at[z_rows], x_v.at[z_rows], x_sem.at[k])

    for k in range(side):
        x_load(k).start()
    y_load = pltpu.make_async_copy(y_hbm.at[pl.ds(pl.multiple_of(me * own, own), own)], rs_res, in_sem.at[1])
    y_load.start()

    def rs_copy(slot, peer):
        return pltpu.make_async_remote_copy(src_ref=u_buf.at[peer], dst_ref=rs_recv.at[slot], send_sem=rs_ssem, recv_sem=rs_rsem,
                                            device_id={"feat": peer}, device_id_type=pl.DeviceIdType.MESH)

    def rs_all():
        return pltpu.make_async_remote_copy(src_ref=u_buf.at[pl.ds(1, n_feat - 1)], dst_ref=rs_recv.at[pl.ds(1, n_feat - 1)],
                                            send_sem=rs_ssem, recv_sem=rs_rsem, device_id={"feat": me},
                                            device_id_type=pl.DeviceIdType.MESH)

    def product_and_send(k):
        pz = (mz + k + 1) % side
        z_rows = pl.ds(pl.multiple_of(pz * zrows, zrows), zrows)
        u = jnp.dot(x_v[z_rows, :], sb[...], preferred_element_type=jnp.float32)
        u_buf[pl.ds(pz * per_z, per_z)] = u.astype(jnp.bfloat16).reshape(per_z, own, targets)
        dz = (k + 1) % side
        for dy in range(side - 1, -1, -1):
            for dx in range(side - 1, -1, -1):
                peer = peer_of(dz, dy, dx)
                slot = dz * side * side + dy * side + dx
                if dy == 0 and dx == 0:
                    @pl.when(dz != 0)
                    def _():
                        rs_copy(slot, peer).start()
                else:
                    rs_copy(slot, peer).start()

    def reduced():
        rs_all().wait_recv()
        acc = u_buf[me].astype(jnp.float32)
        for d in range(1, n_feat):
            acc = acc + rs_recv[d].astype(jnp.float32)
        return acc

    def gather_copies(src_ref, dst_ref):
        out = []
        for d in range(n_feat - 1, 0, -1):
            peer = peer_of(d // (side * side), (d // side) % side, d % side)
            out.append(pltpu.make_async_remote_copy(src_ref=src_ref, dst_ref=dst_ref.at[me], send_sem=ag_ssem, recv_sem=ag_rsem,
                                                    device_id={"feat": peer}, device_id_type=pl.DeviceIdType.MESH))
        return out

    def gather_all(ref):
        part = ref.at[pl.ds(1, n_feat - 1)]
        return pltpu.make_async_remote_copy(src_ref=part, dst_ref=part, send_sem=ag_ssem, recv_sem=ag_rsem, device_id={"feat": me},
                                            device_id_type=pl.DeviceIdType.MESH)

    def g_copy(par, f):
        return pltpu.make_async_remote_copy(src_ref=gt.at[f], dst_ref=g_recv.at[par, f], send_sem=g_ssem.at[f],
                                            recv_sem=g_rsem.at[par, f], device_id={"samp": 1 - core},
                                            device_id_type=pl.DeviceIdType.MESH)

    w_load.wait()
    sb[...] = w_nat[...].astype(jnp.bfloat16)
    x_load(0).wait()
    pl.semaphore_wait(barrier, n_feat)

    def first(k, _):
        @pl.when(k > 0)
        def _():
            x_load(k).wait()
        product_and_send(k)
        return 0

    lax.fori_loop(0, side, first, 0)
    for f in range(n_ft):
        w_t[f] = w_nat[f * FT:(f + 1) * FT, :].T
    lam_t = jnp.broadcast_to(lam_ref[...], (targets, targets)).T
    lam_tile = jnp.concatenate([lam_t] * (FT // targets), axis=1)
    y_load.wait()
    rs_res[...] = rs_res[...] - reduced()
    rs_all().wait_send()

    def sweep(s, _):
        par = s % 2
        rb_full[me] = rs_res[...].astype(jnp.bfloat16)
        for c in gather_copies(rb_full.at[me], rb_full):
            c.start()
        gather_all(rb_full).wait_recv()
        rbt = rb_full[...].reshape(rows, targets).T

        def grad(f, _):
            cols = pl.ds(pl.multiple_of(f * FT, FT), FT)
            gt[f] = jnp.dot(rbt, x_v[:, cols], preferred_element_type=jnp.float32)
            g_copy(par, f).start()
            return 0

        lax.fori_loop(0, n_ft, grad, 0)
        gather_all(rb_full).wait_send()

        def step(f, _):
            g_copy(par, f).wait_recv()
            cols = pl.ds(pl.multiple_of(f * FT, FT), FT)
            gradient = (gt[f] + g_recv[par, f]) / total_rows
            w = w_t[f]
            delta = eta_ref[:, cols] * (gradient - lam_tile * w)
            w_t[f] = w + STEP_WEIGHT * delta
            sb[cols, :] = delta.astype(jnp.bfloat16).T
            return 0

        lax.fori_loop(0, n_ft, step, 0)
        lax.fori_loop(0, side, lambda k, _: (product_and_send(k), 0)[1], 0)
        for f in range(n_ft):
            g_copy(par, f).wait_send()

        @pl.when(s == SWEEPS - 1)
        def _():
            for f in range(n_ft):
                w_nat[f * FT:(f + 1) * FT, :] = w_t[f].T
            pltpu.make_async_copy(w_nat, w_out, out_sem.at[0]).start()

        rs_res[...] = rs_res[...] - STEP_WEIGHT * reduced()
        rs_all().wait_send()
        return 0

    lax.fori_loop(0, SWEEPS, sweep, 0)

    rf_full[me] = rs_res[...]
    for c in gather_copies(rf_full.at[me], rf_full):
        c.start()
    gather_all(rf_full).wait_recv()
    r_copy = pltpu.make_async_copy(rf_full, r_out, out_sem.at[1])
    r_copy.start()
    gather_all(rf_full).wait_send()
    pltpu.make_async_copy(w_nat, w_out, out_sem.at[0]).wait()
    r_copy.wait()


def solution(mesh):
    n_samp, n_feat = mesh.shape["samp"], mesh.shape["feat"]
    side = round(n_feat ** (1 / 3))
    design_spec = P(("problem", "samp"), "feat")
    rows_spec = P(("problem", "samp"), None)
    coef_spec = P(("problem", "feat"), None)
    step_spec = P(("problem", "feat"))
    ridge_spec = P("problem")

    def local_sweeps(design, targets, coef_init, step_sizes, ridge_weights):
        rows, feats = design.shape
        tgt = targets.shape[1]
        own = rows // n_feat
        n_ft = feats // FT
        f32, bf16 = jnp.float32, jnp.bfloat16
        hbm = pl.BlockSpec(memory_space=pl.ANY)
        vmem = pl.BlockSpec(memory_space=pltpu.VMEM)
        w, r = pl.pallas_call(
            functools.partial(_kernel, side, n_feat, n_samp),
            name="descent",
            out_shape=(jax.ShapeDtypeStruct((feats, tgt), f32), jax.ShapeDtypeStruct((n_feat, own, tgt), f32)),
            in_specs=[hbm, hbm, hbm, vmem, vmem],
            out_specs=(hbm, hbm),
            scratch_shapes=[
                pltpu.VMEM((rows, feats), bf16),
                pltpu.VMEM((feats, tgt), f32),
                pltpu.VMEM((n_ft, tgt, FT), f32),
                pltpu.VMEM((feats, tgt), bf16),
                pltpu.VMEM((n_feat, own, tgt), bf16),
                pltpu.VMEM((n_feat, own, tgt), bf16),
                pltpu.VMEM((n_feat, own, tgt), bf16),
                pltpu.VMEM((n_ft, tgt, FT), f32),
                pltpu.VMEM((2, n_ft, tgt, FT), f32),
                pltpu.VMEM((own, tgt), f32),
                pltpu.VMEM((n_feat, own, tgt), f32),
                pltpu.VMEM((own, tgt), f32),
                pltpu.SemaphoreType.DMA((side,)),
                pltpu.SemaphoreType.DMA((2,)),
                pltpu.SemaphoreType.DMA,
                pltpu.SemaphoreType.DMA,
                pltpu.SemaphoreType.DMA,
                pltpu.SemaphoreType.DMA,
                pltpu.SemaphoreType.DMA((n_ft,)),
                pltpu.SemaphoreType.DMA((2, n_ft)),
                pltpu.SemaphoreType.DMA((2,)),
            ],
            compiler_params=pltpu.CompilerParams(collective_id=0, has_side_effects=True, vmem_limit_bytes=56 * 1024 * 1024),
        )(design, targets, coef_init, step_sizes[None, :], ridge_weights[None, :])
        return w, r.reshape(rows, tgt)

    return jax.shard_map(local_sweeps, mesh=mesh, in_specs=(design_spec, rows_spec, coef_spec, step_spec, ridge_spec), out_specs=(coef_spec, rows_spec), check_vma=False)
```

time: 841 us -> 135 us (0.16)
  waiting for transfers between devices: 749 us -> 0 us
  Pallas kernels: 0 us -> 130 us
  matrix products: 66.7 us -> 0 us
  between operations: 13.9 us -> 0.64 us
  other arithmetic: 10.3 us -> 0 us
    psum x9 -> x0, waiting for transfers between devices: 749 us -> none  [the longest x4 528 us: local_sweeps(): lax.psum(block_product(step_delta), 'feat')]
    pallas_call x0 -> x1, Pallas kernels: none -> 130 us  [local_sweeps(): pl.pallas_call(functools.partial(_kernel, side, n_feat, n_samp), name='de...]
    dot_general x9 -> x0, matrix products: 66.7 us -> none  [the longest x5 35.2 us: block_product(): jnp.dot(design, weights.astype(jnp.bfloat16), preferred_element_type=jnp....]
  transfers between devices with their start and end apart: 9 -> 0, of which waited for: 9 -> 0; matrix products, arithmetic and copies ran while one was open for 1% -> 0% of each run, Pallas kernels for 0% -> 0%
where the time goes in v1:
time: 135 us
  Pallas kernels  130 us (96%)
  local copies, waits for them, and re-layouts  4.52 us (3%)
    pallas_call x1, Pallas kernels, local_sweeps(): pl.pallas_call(functools.partial(_kernel, side, n_feat, n_samp), name='de...  130 us
    unnamed x2, local copies, waits for them, and re-layouts  4.52 us

profile of v1, /device:TPU:0, one launch (start us, length us, event | category | flops | bytes accessed | tf_op | source)
XLA Modules:
  0.0 135.2 jit_solution(15981870103579658025)
XLA Ops:
  0.6 130.0 %descent.1 = (f32[2048,128]{1,0:T(8,128)}, f32[64,32,128]{2,1,0:T(8,128)}) custom-call(bf16[2048,2048]{1,0:T(8,128)(2,1)} %x_hbm.1, f32[2048,128]{1,0:T(8,128)} %y_hbm.1, f32[2048,128]{1,0:T(8,128)} %w0_hbm.1, f32[1,2048]{1,0:T(1,128)} %bitcast.4, f32[1,128]{1,0:T(1,128)} %bitcast.5), custom_call_target="tpu_custom_call" | custom-call | tf_op jit(solution)/shard_map/descent/pallas_call | solution.py:195
  130.7 2.3 %copy.9 = f32[2048,128]{1,0:T(8,128)} copy(f32[2048,128]{1,0:T(8,128)} %get-tuple-element.8) | data formatting | bytes 2097152
  132.9 2.3 %copy.10 = f32[2048,128]{1,0:T(8,128)} copy(f32[2048,128]{1,0:T(8,128)} %bitcast.3) | data formatting | bytes 2097152

commit v2 on v0

v2 whole, which is shorter than its diff:
```python
import functools

import jax
import jax.numpy as jnp
from jax import lax
from jax.experimental import pallas as pl
from jax.experimental.pallas import tpu as pltpu
from jax.sharding import PartitionSpec as P

SWEEPS = 4
STEP_WEIGHT = 0.5
CHAINS = 2
TILE = 128
BIG = 512
MESH = pl.DeviceIdType.MESH


def _kernel(n_feat, n_samp, x_hbm, y_hbm, w0_hbm, eta_ref, lam_ref, w_out, r_out,
            x_v, w_nat, w_t, st, u_buf, rs_recv, rb_full, gt, g_recv, rs_res, rf_full, y_tile, lam_t,
            x_sem, in_sem, rs_ssem, rs_rsem, ag_ssem, ag_rsem, g_ssem, g_rsem, out_sem):
    rows, feats = x_v.shape
    targets = w_nat.shape[1]
    half = targets // CHAINS
    n_sg = rows // TILE
    n_tg = n_feat // n_sg
    th = half // n_tg
    n_fb, n_sb = feats // BIG, rows // BIG
    per_sb = n_feat // n_sb
    total_rows = rows * n_samp

    me = lax.axis_index("feat")
    core = lax.axis_index("samp")

    barrier = pltpu.get_barrier_semaphore()

    def greet(d, _):
        pl.semaphore_signal(barrier, inc=1, device_id={"feat": (me + d) % n_feat}, device_id_type=MESH)
        return 0

    lax.fori_loop(1, n_feat, greet, 0)
    pl.semaphore_signal(barrier, inc=1, device_id={"samp": 1 - core}, device_id_type=MESH)

    w_load = pltpu.make_async_copy(w0_hbm, w_nat, in_sem.at[0])
    w_load.start()

    my_sb = me // per_sb

    def block_rows(k):
        return pl.ds(pl.multiple_of(((my_sb + k + 1) % n_sb) * BIG, BIG), BIG)

    def x_load(k):
        return pltpu.make_async_copy(x_hbm.at[block_rows(k)], x_v.at[block_rows(k)], x_sem.at[k])

    for k in range(n_sb):
        x_load(k).start()
    my_sg, my_tg = me // n_tg, me % n_tg
    y_load = pltpu.make_async_copy(y_hbm.at[pl.ds(pl.multiple_of(my_sg * TILE, TILE), TILE)], y_tile, in_sem.at[1])
    y_load.start()

    def rs_copy(c, peer):
        return pltpu.make_async_remote_copy(src_ref=u_buf.at[c, peer], dst_ref=rs_recv.at[c, me], send_sem=rs_ssem.at[c],
                                            recv_sem=rs_rsem.at[c], device_id={"feat": peer}, device_id_type=MESH)

    def rs_all(c):
        return pltpu.make_async_remote_copy(src_ref=u_buf.at[c, pl.ds(1, n_feat - 1)], dst_ref=rs_recv.at[c, pl.ds(1, n_feat - 1)],
                                            send_sem=rs_ssem.at[c], recv_sem=rs_rsem.at[c], device_id={"feat": me},
                                            device_id_type=MESH)

    def product_and_send(c, k):
        sb = (my_sb + k + 1) % n_sb
        u = lax.dot_general(st[c], x_v[block_rows(k), :], (((1,), (1,)), ((), ())), preferred_element_type=jnp.float32)
        for j in range(per_sb):
            g, t = j // n_tg, j % n_tg
            part = u[t * th:(t + 1) * th, g * TILE:(g + 1) * TILE].astype(jnp.bfloat16)
            u_buf[c, sb * per_sb + j] = part
        for i in range(per_sb):
            peer = sb * per_sb + (my_in_sb + i) % per_sb
            if i == 0:
                @pl.when(k != n_sb - 1)
                def _():
                    rs_copy(c, peer).start()
            else:
                rs_copy(c, peer).start()

    my_in_sb = me % per_sb

    def reduce(c, coef):
        rs_all(c).wait_recv()
        rs_recv[c, me] = u_buf[c, me]
        accs = [rs_recv[c, j].astype(jnp.float32) for j in range(4)]
        for j in range(4, n_feat):
            accs[j % 4] = accs[j % 4] + rs_recv[c, j].astype(jnp.float32)
        total = (accs[0] + accs[1]) + (accs[2] + accs[3])
        rs_res[c] = rs_res[c] - coef * total

    def gather_start(c, ref):
        def send(d, _):
            peer = (me + n_feat // 2 + d) % n_feat
            @pl.when(peer != me)
            def _():
                pltpu.make_async_remote_copy(src_ref=ref.at[c, me], dst_ref=ref.at[c, me], send_sem=ag_ssem.at[c],
                                             recv_sem=ag_rsem.at[c], device_id={"feat": peer}, device_id_type=MESH).start()
            return 0
        lax.fori_loop(0, n_feat, send, 0, unroll=8)

    def gather_all(c, ref):
        part = ref.at[c, pl.ds(1, n_feat - 1)]
        return pltpu.make_async_remote_copy(src_ref=part, dst_ref=part, send_sem=ag_ssem.at[c], recv_sem=ag_rsem.at[c],
                                            device_id={"feat": me}, device_id_type=MESH)

    def g_copy(c, par, f):
        return pltpu.make_async_remote_copy(src_ref=gt.at[c, f], dst_ref=g_recv.at[par, c, f], send_sem=g_ssem.at[c, f],
                                            recv_sem=g_rsem.at[par, c, f], device_id={"samp": 1 - core}, device_id_type=MESH)

    w_load.wait()
    for f in range(n_fb):
        wt = w_nat[f * BIG:(f + 1) * BIG, :].T
        for c in range(CHAINS):
            w_t[c, f] = wt[c * half:(c + 1) * half]
            st[c, :, f * BIG:(f + 1) * BIG] = wt[c * half:(c + 1) * half].astype(jnp.bfloat16)
    lam_t[...] = jnp.broadcast_to(lam_ref[...], (targets, targets)).T
    x_load(0).wait()
    pl.semaphore_wait(barrier, n_feat)

    def first(i, _):
        c, k = i // n_sb, i % n_sb
        @pl.when((i > 0) & (i < n_sb))
        def _():
            x_load(k).wait()
        product_and_send(c, k)
        return 0

    lax.fori_loop(0, CHAINS * n_sb, first, 0)
    y_load.wait()
    y_tile[...] = y_tile[...].T

    def first_reduce(c, _):
        rs_res[c] = y_tile[pl.ds(pl.multiple_of(c * half + my_tg * th, th), th), :]
        reduce(c, 1.0)
        rb_full[c, me] = rs_res[c].astype(jnp.bfloat16)
        gather_start(c, rb_full)
        rs_all(c).wait_send()
        return 0

    lax.fori_loop(0, CHAINS, first_reduce, 0)

    def sweep(s, _):
        par = s % 2

        def ahead(c, _):
            gather_all(c, rb_full).wait_recv()
            rbt = jnp.concatenate([rb_full[c, g * n_tg:(g + 1) * n_tg].reshape(half, TILE) for g in range(n_sg)], axis=1)

            def grad(f, _):
                cols = pl.ds(pl.multiple_of(f * BIG, BIG), BIG)
                gt[c, f] = jnp.dot(rbt, x_v[:, cols], preferred_element_type=jnp.float32)
                g_copy(c, par, f).start()
                return 0

            lax.fori_loop(0, n_fb, grad, 0)
            gather_all(c, rb_full).wait_send()
            lam = lam_t[pl.ds(pl.multiple_of(c * half, half), half), :]
            lam = jnp.concatenate([lam] * (BIG // targets), axis=1)

            def step(f, _):
                g_copy(c, par, f).wait_recv()
                cols = pl.ds(pl.multiple_of(f * BIG, BIG), BIG)
                gradient = (gt[c, f] + g_recv[par, c, f]) / total_rows
                w = w_t[c, f]
                delta = eta_ref[:, cols] * (gradient - lam * w)
                w_t[c, f] = w + STEP_WEIGHT * delta
                st[c, :, cols] = delta.astype(jnp.bfloat16)
                return 0

            lax.fori_loop(0, n_fb, step, 0)
            lax.fori_loop(0, n_sb, lambda k, _: (product_and_send(c, k), 0)[1], 0)
            for f in range(n_fb):
                g_copy(c, par, f).wait_send()
            return 0

        lax.fori_loop(0, CHAINS, ahead, 0)

        @pl.when(s == SWEEPS - 1)
        def _():
            for f in range(n_fb):
                w_nat[f * BIG:(f + 1) * BIG, :] = jnp.concatenate([w_t[c, f] for c in range(CHAINS)], axis=0).T
            pltpu.make_async_copy(w_nat, w_out, out_sem.at[0]).start()

        def behind(c, _):
            reduce(c, STEP_WEIGHT)

            @pl.when(s < SWEEPS - 1)
            def _():
                rb_full[c, me] = rs_res[c].astype(jnp.bfloat16)
                gather_start(c, rb_full)

            @pl.when(s == SWEEPS - 1)
            def _():
                rf_full[c, me] = rs_res[c]
                gather_start(c, rf_full)

            rs_all(c).wait_send()
            return 0

        lax.fori_loop(0, CHAINS, behind, 0)
        return 0

    lax.fori_loop(0, SWEEPS, sweep, 0)

    for c in range(CHAINS):
        gather_all(c, rf_full).wait_recv()
    pltpu.make_async_copy(w_nat, w_out, out_sem.at[0]).wait()
    for g in range(n_sg):
        both = jnp.concatenate([rf_full[c, g * n_tg:(g + 1) * n_tg].reshape(half, TILE) for c in range(CHAINS)], axis=0)
        w_nat[g * TILE:(g + 1) * TILE, :] = both.T
    r_copy = pltpu.make_async_copy(w_nat, r_out, out_sem.at[1])
    r_copy.start()
    for c in range(CHAINS):
        gather_all(c, rf_full).wait_send()
    r_copy.wait()


def solution(mesh):
    n_samp, n_feat = mesh.shape["samp"], mesh.shape["feat"]
    design_spec = P(("problem", "samp"), "feat")
    rows_spec = P(("problem", "samp"), None)
    coef_spec = P(("problem", "feat"), None)
    step_spec = P(("problem", "feat"))
    ridge_spec = P("problem")

    def local_sweeps(design, targets, coef_init, step_sizes, ridge_weights):
        rows, feats = design.shape
        tgt = targets.shape[1]
        half = tgt // CHAINS
        n_fb, n_sb = feats // BIG, rows // BIG
        n_tg = n_feat // (rows // TILE)
        th = half // n_tg
        f32, bf16 = jnp.float32, jnp.bfloat16
        hbm = pl.BlockSpec(memory_space=pl.ANY)
        vmem = pl.BlockSpec(memory_space=pltpu.VMEM)
        return pl.pallas_call(
            functools.partial(_kernel, n_feat, n_samp),
            name="descent",
            out_shape=(jax.ShapeDtypeStruct((feats, tgt), f32), jax.ShapeDtypeStruct((rows, tgt), f32)),
            in_specs=[hbm, hbm, hbm, vmem, vmem],
            out_specs=(hbm, hbm),
            scratch_shapes=[
                pltpu.VMEM((rows, feats), bf16),
                pltpu.VMEM((feats, tgt), f32),
                pltpu.VMEM((CHAINS, n_fb, half, BIG), f32),
                pltpu.VMEM((CHAINS, half, feats), bf16),
                pltpu.VMEM((CHAINS, n_feat, th, TILE), bf16),
                pltpu.VMEM((CHAINS, n_feat, th, TILE), bf16),
                pltpu.VMEM((CHAINS, n_feat, th, TILE), bf16),
                pltpu.VMEM((CHAINS, n_fb, half, BIG), f32),
                pltpu.VMEM((2, CHAINS, n_fb, half, BIG), f32),
                pltpu.VMEM((CHAINS, th, TILE), f32),
                pltpu.VMEM((CHAINS, n_feat, th, TILE), f32),
                pltpu.VMEM((TILE, tgt), f32),
                pltpu.VMEM((tgt, tgt), f32),
                pltpu.SemaphoreType.DMA((n_sb,)),
                pltpu.SemaphoreType.DMA((2,)),
                pltpu.SemaphoreType.DMA((CHAINS,)),
                pltpu.SemaphoreType.DMA((CHAINS,)),
                pltpu.SemaphoreType.DMA((CHAINS,)),
                pltpu.SemaphoreType.DMA((CHAINS,)),
                pltpu.SemaphoreType.DMA((CHAINS, n_fb)),
                pltpu.SemaphoreType.DMA((2, CHAINS, n_fb)),
                pltpu.SemaphoreType.DMA((2,)),
            ],
            compiler_params=pltpu.CompilerParams(collective_id=0, has_side_effects=True, vmem_limit_bytes=56 * 1024 * 1024),
        )(design, targets, coef_init, step_sizes[None, :], ridge_weights[None, :])

    return jax.shard_map(local_sweeps, mesh=mesh, in_specs=(design_spec, rows_spec, coef_spec, step_spec, ridge_spec), out_specs=(coef_spec, rows_spec), check_vma=False)
```

time: 841 us -> 124 us (0.15)
  waiting for transfers between devices: 749 us -> 0 us
  Pallas kernels: 0 us -> 119 us
  matrix products: 66.7 us -> 0 us
  between operations: 13.9 us -> 0.64 us
  other arithmetic: 10.3 us -> 0 us
    psum x9 -> x0, waiting for transfers between devices: 749 us -> none  [the longest x4 528 us: local_sweeps(): lax.psum(block_product(step_delta), 'feat')]
    pallas_call x0 -> x1, Pallas kernels: none -> 119 us  [local_sweeps(): pl.pallas_call(functools.partial(_kernel, n_feat, n_samp), name='descent'...]
    dot_general x9 -> x0, matrix products: 66.7 us -> none  [the longest x5 35.2 us: block_product(): jnp.dot(design, weights.astype(jnp.bfloat16), preferred_element_type=jnp....]
  transfers between devices with their start and end apart: 9 -> 0, of which waited for: 9 -> 0; matrix products, arithmetic and copies ran while one was open for 1% -> 0% of each run, Pallas kernels for 0% -> 0%
where the time goes in v2:
time: 124 us
  Pallas kernels  119 us (96%)
  local copies, waits for them, and re-layouts  4.52 us (4%)
    pallas_call x1, Pallas kernels, local_sweeps(): pl.pallas_call(functools.partial(_kernel, n_feat, n_samp), name='descent'...  119 us
    unnamed x2, local copies, waits for them, and re-layouts  4.52 us

profile of v2, /device:TPU:0, one launch (start us, length us, event | category | flops | bytes accessed | tf_op | source)
XLA Modules:
  0.0 124.2 jit_solution(3724067066908636090)
XLA Ops:
  0.6 119.0 %descent.1 = (f32[2048,128]{1,0:T(8,128)}, f32[2048,128]{1,0:T(8,128)}) custom-call(bf16[2048,2048]{1,0:T(8,128)(2,1)} %x_hbm.1, f32[2048,128]{1,0:T(8,128)} %y_hbm.1, f32[2048,128]{1,0:T(8,128)} %w0_hbm.1, f32[1,2048]{1,0:T(1,128)} %bitcast.2, f32[1,128]{1,0:T(1,128)} %bitcast.3), custom_call_target="tpu_custom_call" | custom-call | tf_op jit(solution)/shard_map/descent/pallas_call | solution.py:241
  119.7 2.3 %copy.9 = f32[2048,128]{1,0:T(8,128)} copy(f32[2048,128]{1,0:T(8,128)} %get-tuple-element.4) | data formatting | bytes 2097152
  121.9 2.3 %copy.10 = f32[2048,128]{1,0:T(8,128)} copy(f32[2048,128]{1,0:T(8,128)} %get-tuple-element.5) | data formatting | bytes 2097152

commit v3 on v2

v3 whole, which is shorter than its diff:
```python
import functools

import jax
import jax.numpy as jnp
from jax import lax
from jax.experimental import pallas as pl
from jax.experimental.pallas import tpu as pltpu
from jax.sharding import PartitionSpec as P

SWEEPS = 4
STEP_WEIGHT = 0.5
CHAINS = 2
TILE = 128
BIG = 512
MESH = pl.DeviceIdType.MESH


def _kernel(side, n_feat, n_samp, x_hbm, y_hbm, w0_hbm, eta_ref, lam_ref, w_out, r_out,
            x_v, xt_v, w_nat, w_t, st, u_buf, rs_recv, rb_full, gt, g_recv, rs_res, rf_full, y_tile, lam_t,
            x_sem, in_sem, rs_ssem, rs_rsem, ag_ssem, ag_psem, ag_rsem, g_ssem, g_rsem, out_sem):
    rows, feats = x_v.shape
    targets = w_nat.shape[1]
    half = targets // CHAINS
    n_sg = rows // TILE
    n_tg = n_feat // n_sg
    th = half // n_tg
    n_fb, n_sb = feats // BIG, rows // BIG
    per_sb = n_feat // n_sb
    total_rows = rows * n_samp

    me = lax.axis_index("feat")
    core = lax.axis_index("samp")

    barrier = pltpu.get_barrier_semaphore()

    def greet(d, _):
        pl.semaphore_signal(barrier, inc=1, device_id={"feat": (me + d) % n_feat}, device_id_type=MESH)
        return 0

    lax.fori_loop(1, n_feat, greet, 0)
    pl.semaphore_signal(barrier, inc=1, device_id={"samp": 1 - core}, device_id_type=MESH)

    w_load = pltpu.make_async_copy(w0_hbm, w_nat, in_sem.at[0])
    w_load.start()

    my_sb = me // per_sb

    def block_rows(k):
        return pl.ds(pl.multiple_of(((my_sb + k + 1) % n_sb) * BIG, BIG), BIG)

    def x_load(k):
        return pltpu.make_async_copy(x_hbm.at[block_rows(k)], x_v.at[block_rows(k)], x_sem.at[k])

    for k in range(n_sb):
        x_load(k).start()
    my_sg, my_tg = me // n_tg, me % n_tg
    y_load = pltpu.make_async_copy(y_hbm.at[pl.ds(pl.multiple_of(my_sg * TILE, TILE), TILE)], y_tile, in_sem.at[1])
    y_load.start()

    def rs_copy(c, peer):
        return pltpu.make_async_remote_copy(src_ref=u_buf.at[c, peer], dst_ref=rs_recv.at[c, me], send_sem=rs_ssem.at[c],
                                            recv_sem=rs_rsem.at[c], device_id={"feat": peer}, device_id_type=MESH)

    def rs_all(c):
        return pltpu.make_async_remote_copy(src_ref=u_buf.at[c, pl.ds(1, n_feat - 1)], dst_ref=rs_recv.at[c, pl.ds(1, n_feat - 1)],
                                            send_sem=rs_ssem.at[c], recv_sem=rs_rsem.at[c], device_id={"feat": me},
                                            device_id_type=MESH)

    my_in_sb = me % per_sb

    def send_tiles(c, k, u):
        sb = (my_sb + k + 1) % n_sb
        for j in range(per_sb):
            g, t = j // n_tg, j % n_tg
            u_buf[c, sb * per_sb + j] = u[t * th:(t + 1) * th, g * TILE:(g + 1) * TILE].astype(jnp.bfloat16)
        for i in range(per_sb):
            peer = sb * per_sb + (my_in_sb + i) % per_sb
            if i == 0:
                @pl.when(k != n_sb - 1)
                def _():
                    rs_copy(c, peer).start()
            else:
                rs_copy(c, peer).start()

    def reduce(c, coef):
        rs_all(c).wait_recv()
        rs_recv[c, me] = u_buf[c, me]
        accs = [rs_recv[c, j].astype(jnp.float32) for j in range(4)]
        for j in range(4, n_feat):
            accs[j % 4] = accs[j % 4] + rs_recv[c, j].astype(jnp.float32)
        total = (accs[0] + accs[1]) + (accs[2] + accs[3])
        rs_res[c] = rs_res[c] - coef * total

    def axes(c):
        third = (c * n_samp + core) % 3
        strides = [jnp.where(d == 0, 1, jnp.where(d == 1, side, side * side)) for d in (third, (third + 1) % 3, (third + 2) % 3)]
        return [(stride, (me // stride) % side) for stride in strides]

    def moved(axis, by):
        stride, at = axis
        return ((at + by) % side - at) * stride

    def hops(d):
        return min(d, side - d)

    plane = sorted([(a, b) for a in range(side) for b in range(side) if a or b], key=lambda o: hops(o[0]) + hops(o[1]))

    def pass_on(c, ref, owner):
        ring = axes(c)[0]
        for d in range(side - 1, 0, -1):
            pltpu.make_async_remote_copy(src_ref=ref.at[c, owner], dst_ref=ref.at[c, owner], send_sem=ag_ssem.at[c],
                                         recv_sem=ag_rsem.at[c], device_id={"feat": me + moved(ring, d)}, device_id_type=MESH).start()

    def plane_copy(c, ref, i, owner, peer):
        return pltpu.make_async_remote_copy(src_ref=ref.at[c, owner], dst_ref=ref.at[c, owner], send_sem=ag_ssem.at[c],
                                            recv_sem=ag_psem.at[c, i], device_id={"feat": peer}, device_id_type=MESH)

    def gather_start(c, ref):
        _, one, two = axes(c)
        for i in range(len(plane) - 1, -1, -1):
            a, b = plane[i]
            plane_copy(c, ref, i, me, me + moved(one, a) + moved(two, b)).start()
        pass_on(c, ref, me)

    def gather_forward(c, ref):
        _, one, two = axes(c)
        for i, (a, b) in enumerate(plane):
            owner = me + moved(one, side - a) + moved(two, side - b)
            plane_copy(c, ref, i, owner, me).wait_recv()
            pass_on(c, ref, owner)

    def gather_wait(c, ref):
        part = ref.at[c, pl.ds(0, n_feat - side * side)]
        pltpu.make_async_remote_copy(src_ref=part, dst_ref=part, send_sem=ag_ssem.at[c], recv_sem=ag_rsem.at[c],
                                     device_id={"feat": me}, device_id_type=MESH).wait_recv()

    def gather_sent(c, ref):
        part = ref.at[c, pl.ds(1, n_feat - 1)]
        pltpu.make_async_remote_copy(src_ref=part, dst_ref=part, send_sem=ag_ssem.at[c], recv_sem=ag_rsem.at[c],
                                     device_id={"feat": me}, device_id_type=MESH).wait_send()

    def g_copy(c, par, f):
        return pltpu.make_async_remote_copy(src_ref=gt.at[c, f], dst_ref=g_recv.at[par, c, f], send_sem=g_ssem.at[c, f],
                                            recv_sem=g_rsem.at[par, c, f], device_id={"samp": 1 - core}, device_id_type=MESH)

    w_load.wait()
    for f in range(n_fb):
        wt = w_nat[f * BIG:(f + 1) * BIG, :].T
        for c in range(CHAINS):
            w_t[c, f] = wt[c * half:(c + 1) * half]
            st[c, :, f * BIG:(f + 1) * BIG] = wt[c * half:(c + 1) * half].astype(jnp.bfloat16)
    lam_t[...] = jnp.broadcast_to(lam_ref[...], (targets, targets)).T
    x_load(0).wait()
    pl.semaphore_wait(barrier, n_feat)

    def first(k, _):
        @pl.when(k > 0)
        def _():
            x_load(k).wait()
        u = lax.dot_general(st[...].reshape(targets, feats), x_v[block_rows(k), :], (((1,), (1,)), ((), ())),
                            preferred_element_type=jnp.float32)
        for c in range(CHAINS):
            send_tiles(c, k, u[c * half:(c + 1) * half])
        return 0

    lax.fori_loop(0, n_sb, first, 0)

    def turn(r, _):
        piece = pl.ds(pl.multiple_of(r * TILE, TILE), TILE)
        xt_v[:, piece] = x_v[piece, :].T
        return 0

    lax.fori_loop(0, n_sg, turn, 0)
    y_load.wait()
    y_tile[...] = y_tile[...].T

    def behind(c, coef, last):
        reduce(c, coef)
        if last:
            rf_full[c, me] = rs_res[c]
        else:
            rb_full[c, me] = rs_res[c].astype(jnp.bfloat16)
        gather_start(c, rf_full if last else rb_full)
        rs_all(c).wait_send()

    def gradient_part(c, par):
        gather_wait(c, rb_full)
        rbt = jnp.concatenate([rb_full[c, g * n_tg:(g + 1) * n_tg].reshape(half, TILE) for g in range(n_sg)], axis=1)

        def grad(f, _):
            cols = pl.ds(pl.multiple_of(f * BIG, BIG), BIG)
            gt[c, f] = jnp.dot(rbt, x_v[:, cols], preferred_element_type=jnp.float32)
            g_copy(c, par, f).start()
            return 0

        lax.fori_loop(0, n_fb, grad, 0)

    def step_and_product(c, par):
        lam = lam_t[c * half:(c + 1) * half, :]
        lam = jnp.concatenate([lam] * (BIG // targets), axis=1)

        def step(f, _):
            g_copy(c, par, f).wait_recv()
            cols = pl.ds(pl.multiple_of(f * BIG, BIG), BIG)
            gradient = (gt[c, f] + g_recv[par, c, f]) / total_rows
            w = w_t[c, f]
            delta = eta_ref[:, cols] * (gradient - lam * w)
            w_t[c, f] = w + STEP_WEIGHT * delta
            st[c, :, cols] = delta.astype(jnp.bfloat16)
            return 0

        lax.fori_loop(0, n_fb, step, 0)
        gather_sent(c, rb_full)

        def product(k, _):
            send_tiles(c, k, jnp.dot(st[c], xt_v[:, block_rows(k)], preferred_element_type=jnp.float32))
            return 0

        lax.fori_loop(0, n_sb, product, 0)
        for f in range(n_fb):
            g_copy(c, par, f).wait_send()

    def sweep(s, last):
        par = s % 2
        gradient_part(0, par)
        gather_forward(1, rb_full)
        step_and_product(0, par)
        gradient_part(1, par)
        step_and_product(1, par)
        if last:
            for f in range(n_fb):
                w_nat[f * BIG:(f + 1) * BIG, :] = jnp.concatenate([w_t[c, f] for c in range(CHAINS)], axis=0).T
            pltpu.make_async_copy(w_nat, w_out, out_sem.at[0]).start()
        behind(0, STEP_WEIGHT, last)
        gather_forward(0, rf_full if last else rb_full)
        behind(1, STEP_WEIGHT, last)

    for c in range(CHAINS):
        rs_res[c] = y_tile[pl.ds(pl.multiple_of(c * half + my_tg * th, th), th), :]
    behind(0, 1.0, False)
    gather_forward(0, rb_full)
    behind(1, 1.0, False)
    lax.fori_loop(0, SWEEPS - 1, lambda s, _: (sweep(s, False), 0)[1], 0)
    sweep(SWEEPS - 1, True)
    gather_forward(1, rf_full)

    for c in range(CHAINS):
        gather_wait(c, rf_full)
    pltpu.make_async_copy(w_nat, w_out, out_sem.at[0]).wait()
    for g in range(n_sg):
        both = jnp.concatenate([rf_full[c, g * n_tg:(g + 1) * n_tg].reshape(half, TILE) for c in range(CHAINS)], axis=0)
        w_nat[g * TILE:(g + 1) * TILE, :] = both.T
    r_copy = pltpu.make_async_copy(w_nat, r_out, out_sem.at[1])
    r_copy.start()
    for c in range(CHAINS):
        gather_sent(c, rf_full)
    r_copy.wait()


def solution(mesh):
    n_samp, n_feat = mesh.shape["samp"], mesh.shape["feat"]
    side = round(n_feat ** (1 / 3))
    design_spec = P(("problem", "samp"), "feat")
    rows_spec = P(("problem", "samp"), None)
    coef_spec = P(("problem", "feat"), None)
    step_spec = P(("problem", "feat"))
    ridge_spec = P("problem")

    def local_sweeps(design, targets, coef_init, step_sizes, ridge_weights):
        rows, feats = design.shape
        tgt = targets.shape[1]
        half = tgt // CHAINS
        n_fb, n_sb = feats // BIG, rows // BIG
        n_tg = n_feat // (rows // TILE)
        th = half // n_tg
        f32, bf16 = jnp.float32, jnp.bfloat16
        hbm = pl.BlockSpec(memory_space=pl.ANY)
        vmem = pl.BlockSpec(memory_space=pltpu.VMEM)
        return pl.pallas_call(
            functools.partial(_kernel, side, n_feat, n_samp),
            name="descent",
            out_shape=(jax.ShapeDtypeStruct((feats, tgt), f32), jax.ShapeDtypeStruct((rows, tgt), f32)),
            in_specs=[hbm, hbm, hbm, vmem, vmem],
            out_specs=(hbm, hbm),
            scratch_shapes=[
                pltpu.VMEM((rows, feats), bf16),
                pltpu.VMEM((feats, rows), bf16),
                pltpu.VMEM((feats, tgt), f32),
                pltpu.VMEM((CHAINS, n_fb, half, BIG), f32),
                pltpu.VMEM((CHAINS, half, feats), bf16),
                pltpu.VMEM((CHAINS, n_feat, th, TILE), bf16),
                pltpu.VMEM((CHAINS, n_feat, th, TILE), bf16),
                pltpu.VMEM((CHAINS, n_feat, th, TILE), bf16),
                pltpu.VMEM((CHAINS, n_fb, half, BIG), f32),
                pltpu.VMEM((2, CHAINS, n_fb, half, BIG), f32),
                pltpu.VMEM((CHAINS, th, TILE), f32),
                pltpu.VMEM((CHAINS, n_feat, th, TILE), f32),
                pltpu.VMEM((TILE, tgt), f32),
                pltpu.VMEM((tgt, tgt), f32),
                pltpu.SemaphoreType.DMA((n_sb,)),
                pltpu.SemaphoreType.DMA((2,)),
                pltpu.SemaphoreType.DMA((CHAINS,)),
                pltpu.SemaphoreType.DMA((CHAINS,)),
                pltpu.SemaphoreType.DMA((CHAINS,)),
                pltpu.SemaphoreType.DMA((CHAINS, side * side)),
                pltpu.SemaphoreType.DMA((CHAINS,)),
                pltpu.SemaphoreType.DMA((CHAINS, n_fb)),
                pltpu.SemaphoreType.DMA((2, CHAINS, n_fb)),
                pltpu.SemaphoreType.DMA((2,)),
            ],
            compiler_params=pltpu.CompilerParams(collective_id=0, has_side_effects=True, vmem_limit_bytes=56 * 1024 * 1024),
        )(design, targets, coef_init, step_sizes[None, :], ridge_weights[None, :])

    return jax.shard_map(local_sweeps, mesh=mesh, in_specs=(design_spec, rows_spec, coef_spec, step_spec, ridge_spec), out_specs=(coef_spec, rows_spec), check_vma=False)
```

time: 124 us -> 130 us (1.048)
  Pallas kernels: 119 us -> 124 us
    pallas_call x1, Pallas kernels: 119 us -> 124 us  [local_sweeps(): pl.pallas_call(functools.partial(_kernel, side, n_feat, n_samp), name='de...]
where the time goes in v3:
time: 130 us
  Pallas kernels  124 us (95%)
  local copies, waits for them, and re-layouts  4.52 us (3%)
    pallas_call x1, Pallas kernels, local_sweeps(): pl.pallas_call(functools.partial(_kernel, side, n_feat, n_samp), name='de...  124 us
    unnamed x2, local copies, waits for them, and re-layouts  4.52 us

profile of v3, /device:TPU:0, one launch (start us, length us, event | category | flops | bytes accessed | tf_op | source)
XLA Modules:
  0.0 129.6 jit_solution(15050356010570692200)
XLA Ops:
  0.6 124.4 %descent.1 = (f32[2048,128]{1,0:T(8,128)}, f32[2048,128]{1,0:T(8,128)}) custom-call(bf16[2048,2048]{1,0:T(8,128)(2,1)} %x_hbm.1, f32[2048,128]{1,0:T(8,128)} %y_hbm.1, f32[2048,128]{1,0:T(8,128)} %w0_hbm.1, f32[1,2048]{1,0:T(1,128)} %bitcast.2, f32[1,128]{1,0:T(1,128)} %bitcast.3), custom_call_target="tpu_custom_call" | custom-call | tf_op jit(solution)/shard_map/descent/pallas_call | solution.py:279
  125.1 2.3 %copy.9 = f32[2048,128]{1,0:T(8,128)} copy(f32[2048,128]{1,0:T(8,128)} %get-tuple-element.4) | data formatting | bytes 2097152
  127.3 2.3 %copy.10 = f32[2048,128]{1,0:T(8,128)} copy(f32[2048,128]{1,0:T(8,128)} %get-tuple-element.5) | data formatting | bytes 2097152

commit v4 on v3

--- a/solution.py
+++ b/solution.py
@@ -25,6 +25,14 @@
     n_tg = n_feat // n_sg
     th = half // n_tg
     n_fb, n_sb = feats // BIG, rows // BIG
+
+    def hops(*by):
+        return sum(min(d, side - d) for d in by)
+
+    steps = range(side)
+    plane = sorted([(a, b) for a in steps for b in steps if a or b], key=lambda o: hops(*o))
+    far_first = sorted([(a, b, d) for a in steps for b in steps for d in steps if a or b or d],
+                       key=lambda o: (-hops(*o), (o[0] + 3 * o[1] + 5 * o[2]) % 7))
     per_sb = n_feat // n_sb
     total_rows = rows * n_samp
 
@@ -43,7 +51,9 @@
     w_load = pltpu.make_async_copy(w0_hbm, w_nat, in_sem.at[0])
     w_load.start()
 
-    my_sb = me // per_sb
+    mz, my, mx = me // (side * side), (me // side) % side, me % side
+    my_sb, my_in_sb = (mx + my + mz) % side, mz * side + my
+    pos = my_sb * per_sb + my_in_sb
 
     def block_rows(k):
         return pl.ds(pl.multiple_of(((my_sb + k + 1) % n_sb) * BIG, BIG), BIG)
@@ -53,12 +63,12 @@
 
     for k in range(n_sb):
         x_load(k).start()
-    my_sg, my_tg = me // n_tg, me % n_tg
+    my_sg, my_tg = pos // n_tg, pos % n_tg
     y_load = pltpu.make_async_copy(y_hbm.at[pl.ds(pl.multiple_of(my_sg * TILE, TILE), TILE)], y_tile, in_sem.at[1])
     y_load.start()
 
-    def rs_copy(c, peer):
-        return pltpu.make_async_remote_copy(src_ref=u_buf.at[c, peer], dst_ref=rs_recv.at[c, me], send_sem=rs_ssem.at[c],
+    def rs_copy(c, place, peer):
+        return pltpu.make_async_remote_copy(src_ref=u_buf.at[c, place], dst_ref=rs_recv.at[c, pos], send_sem=rs_ssem.at[c],
                                             recv_sem=rs_rsem.at[c], device_id={"feat": peer}, device_id_type=MESH)
 
     def rs_all(c):
@@ -66,71 +76,77 @@
                                             send_sem=rs_ssem.at[c], recv_sem=rs_rsem.at[c], device_id={"feat": me},
                                             device_id_type=MESH)
 
-    my_in_sb = me % per_sb
-
     def send_tiles(c, k, u):
         sb = (my_sb + k + 1) % n_sb
+
+        def send(dz, dy, when):
+            z, y = (mz + dz) % side, (my + dy) % side
+            x = (sb + 2 * side - z - y) % side
+            copy = rs_copy(c, sb * per_sb + z * side + y, z * side * side + y * side + x)
+            if when is True:
+                copy.start()
+            else:
+                pl.when(when)(copy.start)
+
         for j in range(per_sb):
             g, t = j // n_tg, j % n_tg
             u_buf[c, sb * per_sb + j] = u[t * th:(t + 1) * th, g * TILE:(g + 1) * TILE].astype(jnp.bfloat16)
-        for i in range(per_sb):
-            peer = sb * per_sb + (my_in_sb + i) % per_sb
-            if i == 0:
-                @pl.when(k != n_sb - 1)
-                def _():
-                    rs_copy(c, peer).start()
-            else:
-                rs_copy(c, peer).start()
+        for a, b in reversed(plane):
+            send(a, b, True)
+        send(0, 0, k != n_sb - 1)
 
     def reduce(c, coef):
         rs_all(c).wait_recv()
-        rs_recv[c, me] = u_buf[c, me]
+        rs_recv[c, pos] = u_buf[c, pos]
         accs = [rs_recv[c, j].astype(jnp.float32) for j in range(4)]
         for j in range(4, n_feat):
             accs[j % 4] = accs[j % 4] + rs_recv[c, j].astype(jnp.float32)
         total = (accs[0] + accs[1]) + (accs[2] + accs[3])
         rs_res[c] = rs_res[c] - coef * total
 
-    def axes(c):
-        third = (c * n_samp + core) % 3
-        strides = [jnp.where(d == 0, 1, jnp.where(d == 1, side, side * side)) for d in (third, (third + 1) % 3, (third + 2) % 3)]
+    def place_of(device):
+        z, y, x = device // (side * side), (device // side) % side, device % side
+        return (x + y + z) % side * per_sb + z * side + y
+
+    def axes(first_axis):
+        kinds = (first_axis, (first_axis + 1) % 3, (first_axis + 2) % 3)
+        strides = [jnp.where(d == 0, 1, jnp.where(d == 1, side, side * side)) for d in kinds]
         return [(stride, (me // stride) % side) for stride in strides]
 
     def moved(axis, by):
         stride, at = axis
         return ((at + by) % side - at) * stride
 
-    def hops(d):
-        return min(d, side - d)
-
-    plane = sorted([(a, b) for a in range(side) for b in range(side) if a or b], key=lambda o: hops(o[0]) + hops(o[1]))
-
-    def pass_on(c, ref, owner):
-        ring = axes(c)[0]
+    def gather_copy(c, ref, place, peer, recv_sem):
+        return pltpu.make_async_remote_copy(src_ref=ref.at[c, place], dst_ref=ref.at[c, place], send_sem=ag_ssem.at[c],
+                                            recv_sem=recv_sem, device_id={"feat": peer}, device_id_type=MESH)
+
+    def gather_start(c):
+        moves = [[moved(axis, by) for by in range(side)] for axis in axes(core % 3)]
+        for a, b, d in far_first:
+            gather_copy(c, rb_full, pos, me + moves[0][a] + moves[1][b] + moves[2][d], ag_rsem.at[c]).start()
+
+    def pass_on(c, place):
+        ring = axes((c * n_samp + core) % 3)[0]
         for d in range(side - 1, 0, -1):
-            pltpu.make_async_remote_copy(src_ref=ref.at[c, owner], dst_ref=ref.at[c, owner], send_sem=ag_ssem.at[c],
-                                         recv_sem=ag_rsem.at[c], device_id={"feat": me + moved(ring, d)}, device_id_type=MESH).start()
-
-    def plane_copy(c, ref, i, owner, peer):
-        return pltpu.make_async_remote_copy(src_ref=ref.at[c, owner], dst_ref=ref.at[c, owner], send_sem=ag_ssem.at[c],
-                                            recv_sem=ag_psem.at[c, i], device_id={"feat": peer}, device_id_type=MESH)
-
-    def gather_start(c, ref):
-        _, one, two = axes(c)
+            gather_copy(c, rf_full, place, me + moved(ring, d), ag_rsem.at[c]).start()
+
+    def last_gather_start(c):
+        _, one, two = axes((c * n_samp + core) % 3)
         for i in range(len(plane) - 1, -1, -1):
             a, b = plane[i]
-            plane_copy(c, ref, i, me, me + moved(one, a) + moved(two, b)).start()
-        pass_on(c, ref, me)
-
-    def gather_forward(c, ref):
-        _, one, two = axes(c)
+            gather_copy(c, rf_full, pos, me + moved(one, a) + moved(two, b), ag_psem.at[c, i]).start()
+        pass_on(c, pos)
+
+    def last_gather_forward(c):
+        _, one, two = axes((c * n_samp + core) % 3)
         for i, (a, b) in enumerate(plane):
-            owner = me + moved(one, side - a) + moved(two, side - b)
-            plane_copy(c, ref, i, owner, me).wait_recv()
-            pass_on(c, ref, owner)
-
-    def gather_wait(c, ref):
-        part = ref.at[c, pl.ds(0, n_feat - side * side)]
+            place = place_of(me + moved(one, side - a) + moved(two, side - b))
+            gather_copy(c, rf_full, place, me, ag_psem.at[c, i]).wait_recv()
+            pass_on(c, place)
+
+    def gather_wait(c, ref, tiles):
+        part = ref.at[c, pl.ds(0, tiles)]
         pltpu.make_async_remote_copy(src_ref=part, dst_ref=part, send_sem=ag_ssem.at[c], recv_sem=ag_rsem.at[c],
                                      device_id={"feat": me}, device_id_type=MESH).wait_recv()
 
@@ -177,14 +193,15 @@
     def behind(c, coef, last):
         reduce(c, coef)
         if last:
-            rf_full[c, me] = rs_res[c]
+            rf_full[c, pos] = rs_res[c]
+            last_gather_start(c)
         else:
-            rb_full[c, me] = rs_res[c].astype(jnp.bfloat16)
-        gather_start(c, rf_full if last else rb_full)
+            rb_full[c, pos] = rs_res[c].astype(jnp.bfloat16)
+            gather_start(c)
         rs_all(c).wait_send()
 
     def gradient_part(c, par):
-        gather_wait(c, rb_full)
+        gather_wait(c, rb_full, n_feat - 1)
         rbt = jnp.concatenate([rb_full[c, g * n_tg:(g + 1) * n_tg].reshape(half, TILE) for g in range(n_sg)], axis=1)
 
         def grad(f, _):
@@ -223,29 +240,27 @@
     def sweep(s, last):
         par = s % 2
         gradient_part(0, par)
-        gather_forward(1, rb_full)
+        behind(1, jnp.where(s == 0, 1.0, STEP_WEIGHT), False)
         step_and_product(0, par)
         gradient_part(1, par)
+        behind(0, STEP_WEIGHT, last)
         step_and_product(1, par)
         if last:
             for f in range(n_fb):
                 w_nat[f * BIG:(f + 1) * BIG, :] = jnp.concatenate([w_t[c, f] for c in range(CHAINS)], axis=0).T
             pltpu.make_async_copy(w_nat, w_out, out_sem.at[0]).start()
-        behind(0, STEP_WEIGHT, last)
-        gather_forward(0, rf_full if last else rb_full)
-        behind(1, STEP_WEIGHT, last)
+            last_gather_forward(0)
+            behind(1, STEP_WEIGHT, True)
+            last_gather_forward(1)
 
     for c in range(CHAINS):
         rs_res[c] = y_tile[pl.ds(pl.multiple_of(c * half + my_tg * th, th), th), :]
     behind(0, 1.0, False)
-    gather_forward(0, rb_full)
-    behind(1, 1.0, False)
     lax.fori_loop(0, SWEEPS - 1, lambda s, _: (sweep(s, False), 0)[1], 0)
     sweep(SWEEPS - 1, True)
-    gather_forward(1, rf_full)
 
     for c in range(CHAINS):
-        gather_wait(c, rf_full)
+        gather_wait(c, rf_full, n_feat - side * side)
     pltpu.make_async_copy(w_nat, w_out, out_sem.at[0]).wait()
     for g in range(n_sg):
         both = jnp.concatenate([rf_full[c, g * n_tg:(g + 1) * n_tg].reshape(half, TILE) for c in range(CHAINS)], axis=0)

time: 130 us -> 120 us (0.923)
  Pallas kernels: 124 us -> 115 us
    pallas_call x1, Pallas kernels: 124 us -> 115 us  [local_sweeps(): pl.pallas_call(functools.partial(_kernel, side, n_feat, n_samp), name='de...]
where the time goes in v4:
time: 120 us
  Pallas kernels  115 us (96%)
  local copies, waits for them, and re-layouts  4.52 us (4%)
    pallas_call x1, Pallas kernels, local_sweeps(): pl.pallas_call(functools.partial(_kernel, side, n_feat, n_samp), name='de...  115 us
    unnamed x2, local copies, waits for them, and re-layouts  4.52 us

profile of v4, /device:TPU:0, one launch (start us, length us, event | category | flops | bytes accessed | tf_op | source)
XLA Modules:
  0.0 120.0 jit_solution(17176217557256073943)
XLA Ops:
  0.6 114.8 %descent.1 = (f32[2048,128]{1,0:T(8,128)}, f32[2048,128]{1,0:T(8,128)}) custom-call(bf16[2048,2048]{1,0:T(8,128)(2,1)} %x_hbm.1, f32[2048,128]{1,0:T(8,128)} %y_hbm.1, f32[2048,128]{1,0:T(8,128)} %w0_hbm.1, f32[1,2048]{1,0:T(1,128)} %bitcast.2, f32[1,128]{1,0:T(1,128)} %bitcast.3), custom_call_target="tpu_custom_call" | custom-call | tf_op jit(solution)/shard_map/descent/pallas_call | solution.py:294
  115.4 2.3 %copy.9 = f32[2048,128]{1,0:T(8,128)} copy(f32[2048,128]{1,0:T(8,128)} %get-tuple-element.4) | data formatting | bytes 2097152
  117.7 2.3 %copy.10 = f32[2048,128]{1,0:T(8,128)} copy(f32[2048,128]{1,0:T(8,128)} %get-tuple-element.5) | data formatting | bytes 2097152

commit v5 on v4

--- a/solution.py
+++ b/solution.py
@@ -12,12 +12,13 @@
 CHAINS = 2
 TILE = 128
 BIG = 512
+MXU = 256
 MESH = pl.DeviceIdType.MESH
 
 
 def _kernel(side, n_feat, n_samp, x_hbm, y_hbm, w0_hbm, eta_ref, lam_ref, w_out, r_out,
             x_v, xt_v, w_nat, w_t, st, u_buf, rs_recv, rb_full, gt, g_recv, rs_res, rf_full, y_tile, lam_t,
-            x_sem, in_sem, rs_ssem, rs_rsem, ag_ssem, ag_psem, ag_rsem, g_ssem, g_rsem, out_sem):
+            x_sem, in_sem, rs_ssem, rs_rsem, ag_ssem, ag_psem, ag_rsem, g_ssem, g_rsem):
     rows, feats = x_v.shape
     targets = w_nat.shape[1]
     half = targets // CHAINS
@@ -181,12 +182,16 @@
 
     lax.fori_loop(0, n_sb, first, 0)
 
+    eye = (lax.broadcasted_iota(jnp.int32, (MXU, MXU), 0) == lax.broadcasted_iota(jnp.int32, (MXU, MXU), 1)).astype(jnp.bfloat16)
+
     def turn(r, _):
-        piece = pl.ds(pl.multiple_of(r * TILE, TILE), TILE)
-        xt_v[:, piece] = x_v[piece, :].T
+        piece = pl.ds(pl.multiple_of(r * MXU, MXU), MXU)
+        for f in range(0, feats, MXU):
+            turned = lax.dot_general(eye, x_v[piece, f:f + MXU], (((1,), (1,)), ((), ())), preferred_element_type=jnp.float32)
+            xt_v[f:f + MXU, piece] = turned.astype(jnp.bfloat16)
         return 0
 
-    lax.fori_loop(0, n_sg, turn, 0)
+    lax.fori_loop(0, rows // MXU // 2, turn, 0)
     y_load.wait()
     y_tile[...] = y_tile[...].T
 
@@ -247,8 +252,7 @@
         step_and_product(1, par)
         if last:
             for f in range(n_fb):
-                w_nat[f * BIG:(f + 1) * BIG, :] = jnp.concatenate([w_t[c, f] for c in range(CHAINS)], axis=0).T
-            pltpu.make_async_copy(w_nat, w_out, out_sem.at[0]).start()
+                w_out[f * BIG:(f + 1) * BIG, :] = jnp.concatenate([w_t[c, f] for c in range(CHAINS)], axis=0).T
             last_gather_forward(0)
             behind(1, STEP_WEIGHT, True)
             last_gather_forward(1)
@@ -256,20 +260,25 @@
     for c in range(CHAINS):
         rs_res[c] = y_tile[pl.ds(pl.multiple_of(c * half + my_tg * th, th), th), :]
     behind(0, 1.0, False)
+    lax.fori_loop(rows // MXU // 2, rows // MXU, turn, 0)
     lax.fori_loop(0, SWEEPS - 1, lambda s, _: (sweep(s, False), 0)[1], 0)
     sweep(SWEEPS - 1, True)
 
     for c in range(CHAINS):
         gather_wait(c, rf_full, n_feat - side * side)
-    pltpu.make_async_copy(w_nat, w_out, out_sem.at[0]).wait()
     for g in range(n_sg):
         both = jnp.concatenate([rf_full[c, g * n_tg:(g + 1) * n_tg].reshape(half, TILE) for c in range(CHAINS)], axis=0)
-        w_nat[g * TILE:(g + 1) * TILE, :] = both.T
-    r_copy = pltpu.make_async_copy(w_nat, r_out, out_sem.at[1])
-    r_copy.start()
+        r_out[g * TILE:(g + 1) * TILE, :] = both.T
     for c in range(CHAINS):
         gather_sent(c, rf_full)
-    r_copy.wait()
+
+
+def _write(w_ref, r_ref, w_out, r_out, sem):
+    copies = [pltpu.make_async_copy(w_ref, w_out, sem.at[0]), pltpu.make_async_copy(r_ref, r_out, sem.at[1])]
+    for copy in copies:
+        copy.start()
+    for copy in copies:
+        copy.wait()
 
 
 def solution(mesh):
@@ -291,12 +300,12 @@
         f32, bf16 = jnp.float32, jnp.bfloat16
         hbm = pl.BlockSpec(memory_space=pl.ANY)
         vmem = pl.BlockSpec(memory_space=pltpu.VMEM)
-        return pl.pallas_call(
+        w, r = pl.pallas_call(
             functools.partial(_kernel, side, n_feat, n_samp),
             name="descent",
-            out_shape=(jax.ShapeDtypeStruct((feats, tgt), f32), jax.ShapeDtypeStruct((rows, tgt), f32)),
+            out_shape=(pltpu.VMEM((feats, tgt), f32), pltpu.VMEM((rows, tgt), f32)),
             in_specs=[hbm, hbm, hbm, vmem, vmem],
-            out_specs=(hbm, hbm),
+            out_specs=(vmem, vmem),
             scratch_shapes=[
                 pltpu.VMEM((rows, feats), bf16),
                 pltpu.VMEM((feats, rows), bf16),
@@ -321,9 +330,16 @@
                 pltpu.SemaphoreType.DMA((CHAINS,)),
                 pltpu.SemaphoreType.DMA((CHAINS, n_fb)),
                 pltpu.SemaphoreType.DMA((2, CHAINS, n_fb)),
-                pltpu.SemaphoreType.DMA((2,)),
             ],
             compiler_params=pltpu.CompilerParams(collective_id=0, has_side_effects=True, vmem_limit_bytes=56 * 1024 * 1024),
         )(design, targets, coef_init, step_sizes[None, :], ridge_weights[None, :])
+        return pl.pallas_call(
+            _write,
+            name="write",
+            out_shape=(jax.ShapeDtypeStruct(w.shape, f32), jax.ShapeDtypeStruct(r.shape, f32)),
+            in_specs=[vmem, vmem],
+            out_specs=(hbm, hbm),
+            scratch_shapes=[pltpu.SemaphoreType.DMA((2,))],
+        )(pltpu.with_memory_space_constraint(w, pltpu.VMEM), pltpu.with_memory_space_constraint(r, pltpu.VMEM))
 
     return jax.shard_map(local_sweeps, mesh=mesh, in_specs=(design_spec, rows_spec, coef_spec, step_spec, ridge_spec), out_specs=(coef_spec, rows_spec), check_vma=False)

time: 120 us -> 116 us (0.967)
  local copies, waits for them, and re-layouts: 4.52 us -> 0 us
    unnamed x2 -> x0, local copies, waits for them, and re-layouts: 4.52 us -> none
    pallas_call x0 -> x1, Pallas kernels: none -> 1.33 us  [local_sweeps(): pl.pallas_call(_write, name='write', out_shape=(jax.ShapeDtypeStruct(w.sh...]
where the time goes in v5:
time: 116 us
  Pallas kernels  115 us (99%)
    pallas_call x1, Pallas kernels, local_sweeps(): pl.pallas_call(functools.partial(_kernel, side, n_feat, n_samp), name='de...  114 us

profile of v5, /device:TPU:0, one launch (start us, length us, event | category | flops | bytes accessed | tf_op | source)
XLA Modules:
  0.0 115.7 jit_solution(10970692397373236539)
XLA Ops:
  0.6 113.8 %descent.1 = (f32[2048,128]{1,0:T(8,128)S(1)}, f32[2048,128]{1,0:T(8,128)S(1)}) custom-call(bf16[2048,2048]{1,0:T(8,128)(2,1)} %x_hbm.1, f32[2048,128]{1,0:T(8,128)} %y_hbm.1, f32[2048,128]{1,0:T(8,128)} %w0_hbm.1, f32[1,2048]{1,0:T(1,128)} %bitcast.2, f32[1,128]{1,0:T(1,128)} %bitcast.3), custom_call_target="tpu_custom_call" | custom-call | tf_op jit(solution)/shard_map/descent/pallas_call | solution.py:303
  114.4 1.3 %write.1 = (f32[2048,128]{1,0:T(8,128)}, f32[2048,128]{1,0:T(8,128)}) custom-call(f32[2048,128]{1,0:T(8,128)S(1)} %get-tuple-element.4.w_ref, f32[2048,128]{1,0:T(8,128)S(1)} %get-tuple-element.5.r_ref), custom_call_target="tpu_custom_call" | custom-call | tf_op jit(solution)/shard_map/write/pallas_call | solution.py:336

commit v6 on v5

--- a/solution.py
+++ b/solution.py
@@ -77,7 +77,13 @@
                                             send_sem=rs_ssem.at[c], recv_sem=rs_rsem.at[c], device_id={"feat": me},
                                             device_id_type=MESH)
 
-    def send_tiles(c, k, u):
+    def keep_tiles(c, k, u):
+        sb = (my_sb + k + 1) % n_sb
+        for j in range(per_sb):
+            g, t = j // n_tg, j % n_tg
+            u_buf[c, sb * per_sb + j] = u[t * th:(t + 1) * th, g * TILE:(g + 1) * TILE].astype(jnp.bfloat16)
+
+    def send_tiles(c, k):
         sb = (my_sb + k + 1) % n_sb
 
         def send(dz, dy, when):
@@ -89,9 +95,6 @@
             else:
                 pl.when(when)(copy.start)
 
-        for j in range(per_sb):
-            g, t = j // n_tg, j % n_tg
-            u_buf[c, sb * per_sb + j] = u[t * th:(t + 1) * th, g * TILE:(g + 1) * TILE].astype(jnp.bfloat16)
         for a, b in reversed(plane):
             send(a, b, True)
         send(0, 0, k != n_sb - 1)
@@ -177,10 +180,12 @@
         u = lax.dot_general(st[...].reshape(targets, feats), x_v[block_rows(k), :], (((1,), (1,)), ((), ())),
                             preferred_element_type=jnp.float32)
         for c in range(CHAINS):
-            send_tiles(c, k, u[c * half:(c + 1) * half])
+            keep_tiles(c, k, u[c * half:(c + 1) * half])
+        send_tiles(0, k)
         return 0
 
     lax.fori_loop(0, n_sb, first, 0)
+    lax.fori_loop(0, n_sb, lambda k, _: (send_tiles(1, k), 0)[1], 0)
 
     eye = (lax.broadcasted_iota(jnp.int32, (MXU, MXU), 0) == lax.broadcasted_iota(jnp.int32, (MXU, MXU), 1)).astype(jnp.bfloat16)
 
@@ -235,7 +240,8 @@
         gather_sent(c, rb_full)
 
         def product(k, _):
-            send_tiles(c, k, jnp.dot(st[c], xt_v[:, block_rows(k)], preferred_element_type=jnp.float32))
+            keep_tiles(c, k, jnp.dot(st[c], xt_v[:, block_rows(k)], preferred_element_type=jnp.float32))
+            send_tiles(c, k)
             return 0
 
         lax.fori_loop(0, n_sb, product, 0)
@@ -244,25 +250,25 @@
 
     def sweep(s, last):
         par = s % 2
-        gradient_part(0, par)
-        behind(1, jnp.where(s == 0, 1.0, STEP_WEIGHT), False)
-        step_and_product(0, par)
-        gradient_part(1, par)
-        behind(0, STEP_WEIGHT, last)
-        step_and_product(1, par)
+        for c in range(CHAINS):
+            gradient_part(c, par)
+        for c in range(CHAINS):
+            step_and_product(c, par)
         if last:
             for f in range(n_fb):
                 w_out[f * BIG:(f + 1) * BIG, :] = jnp.concatenate([w_t[c, f] for c in range(CHAINS)], axis=0).T
-            last_gather_forward(0)
-            behind(1, STEP_WEIGHT, True)
-            last_gather_forward(1)
+        for c in range(CHAINS):
+            behind(c, STEP_WEIGHT, last)
 
     for c in range(CHAINS):
         rs_res[c] = y_tile[pl.ds(pl.multiple_of(c * half + my_tg * th, th), th), :]
-    behind(0, 1.0, False)
+    for c in range(CHAINS):
+        behind(c, 1.0, False)
     lax.fori_loop(rows // MXU // 2, rows // MXU, turn, 0)
     lax.fori_loop(0, SWEEPS - 1, lambda s, _: (sweep(s, False), 0)[1], 0)
     sweep(SWEEPS - 1, True)
+    for c in range(CHAINS):
+        last_gather_forward(c)
 
     for c in range(CHAINS):
         gather_wait(c, rf_full, n_feat - side * side)

time: 116 us -> 112 us (0.966)
  Pallas kernels: 115 us -> 111 us
    pallas_call x1, Pallas kernels: 114 us -> 110 us  [local_sweeps(): pl.pallas_call(functools.partial(_kernel, side, n_feat, n_samp), name='de...]
where the time goes in v6:
time: 112 us
  Pallas kernels  111 us (99%)
    pallas_call x1, Pallas kernels, local_sweeps(): pl.pallas_call(functools.partial(_kernel, side, n_feat, n_samp), name='de...  110 us

profile of v6, /device:TPU:0, one launch (start us, length us, event | category | flops | bytes accessed | tf_op | source)
XLA Modules:
  0.0 111.5 jit_solution(11916727649604399926)
XLA Ops:
  0.6 109.5 %descent.1 = (f32[2048,128]{1,0:T(8,128)S(1)}, f32[2048,128]{1,0:T(8,128)S(1)}) custom-call(bf16[2048,2048]{1,0:T(8,128)(2,1)} %x_hbm.1, f32[2048,128]{1,0:T(8,128)} %y_hbm.1, f32[2048,128]{1,0:T(8,128)} %w0_hbm.1, f32[1,2048]{1,0:T(1,128)} %bitcast.2, f32[1,128]{1,0:T(1,128)} %bitcast.3), custom_call_target="tpu_custom_call" | custom-call | tf_op jit(solution)/shard_map/descent/pallas_call | solution.py:309
  110.2 1.3 %write.1 = (f32[2048,128]{1,0:T(8,128)}, f32[2048,128]{1,0:T(8,128)}) custom-call(f32[2048,128]{1,0:T(8,128)S(1)} %get-tuple-element.4.w_ref, f32[2048,128]{1,0:T(8,128)S(1)} %get-tuple-element.5.r_ref), custom_call_target="tpu_custom_call" | custom-call | tf_op jit(solution)/shard_map/write/pallas_call | solution.py:342

commit v7 on v6

--- a/solution.py
+++ b/solution.py
@@ -170,17 +170,17 @@
             w_t[c, f] = wt[c * half:(c + 1) * half]
             st[c, :, f * BIG:(f + 1) * BIG] = wt[c * half:(c + 1) * half].astype(jnp.bfloat16)
     lam_t[...] = jnp.broadcast_to(lam_ref[...], (targets, targets)).T
-    x_load(0).wait()
-    pl.semaphore_wait(barrier, n_feat)
 
     def first(k, _):
-        @pl.when(k > 0)
-        def _():
-            x_load(k).wait()
+        x_load(k).wait()
         u = lax.dot_general(st[...].reshape(targets, feats), x_v[block_rows(k), :], (((1,), (1,)), ((), ())),
                             preferred_element_type=jnp.float32)
         for c in range(CHAINS):
             keep_tiles(c, k, u[c * half:(c + 1) * half])
+
+        @pl.when(k == 0)
+        def _():
+            pl.semaphore_wait(barrier, n_feat)
         send_tiles(0, k)
         return 0
 
@@ -252,7 +252,6 @@
         par = s % 2
         for c in range(CHAINS):
             gradient_part(c, par)
-        for c in range(CHAINS):
             step_and_product(c, par)
         if last:
             for f in range(n_fb):

time: 112 us -> 111 us (level)
  no operation moved by 1% of the time
where the time goes in v7:
time: 111 us
  Pallas kernels  111 us (100%)
    pallas_call x1, Pallas kernels, local_sweeps(): pl.pallas_call(functools.partial(_kernel, side, n_feat, n_samp), name='de...  109 us

profile of v7, /device:TPU:0, one launch (start us, length us, event | category | flops | bytes accessed | tf_op | source)
XLA Modules:
  0.0 111.3 jit_solution(3696133940185288387)
XLA Ops:
  0.6 109.4 %descent.1 = (f32[2048,128]{1,0:T(8,128)S(1)}, f32[2048,128]{1,0:T(8,128)S(1)}) custom-call(bf16[2048,2048]{1,0:T(8,128)(2,1)} %x_hbm.1, f32[2048,128]{1,0:T(8,128)} %y_hbm.1, f32[2048,128]{1,0:T(8,128)} %w0_hbm.1, f32[1,2048]{1,0:T(1,128)} %bitcast.2, f32[1,128]{1,0:T(1,128)} %bitcast.3), custom_call_target="tpu_custom_call" | custom-call | tf_op jit(solution)/shard_map/descent/pallas_call | solution.py:308
  110.0 1.3 %write.1 = (f32[2048,128]{1,0:T(8,128)}, f32[2048,128]{1,0:T(8,128)}) custom-call(f32[2048,128]{1,0:T(8,128)S(1)} %get-tuple-element.4.w_ref, f32[2048,128]{1,0:T(8,128)S(1)} %get-tuple-element.5.r_ref), custom_call_target="tpu_custom_call" | custom-call | tf_op jit(solution)/shard_map/write/pallas_call | solution.py:341

commit v8 on v7

--- a/solution.py
+++ b/solution.py
@@ -34,6 +34,7 @@
     plane = sorted([(a, b) for a in steps for b in steps if a or b], key=lambda o: hops(*o))
     far_first = sorted([(a, b, d) for a in steps for b in steps for d in steps if a or b or d],
                        key=lambda o: (-hops(*o), (o[0] + 3 * o[1] + 5 * o[2]) % 7))
+    arrive = sorted(steps, key=lambda q: max(hops(*o) for o in far_first if sum(o) % side == q))
     per_sb = n_feat // n_sb
     total_rows = rows * n_samp
 
@@ -56,17 +57,21 @@
     my_sb, my_in_sb = (mx + my + mz) % side, mz * side + my
     pos = my_sb * per_sb + my_in_sb
 
+    def class_of(k):
+        return sum(jnp.where(k == i, q, 0) for i, q in enumerate(reversed(arrive)))
+
+    def block_of(k):
+        return (my_sb + class_of(k)) % n_sb
+
     def block_rows(k):
-        return pl.ds(pl.multiple_of(((my_sb + k + 1) % n_sb) * BIG, BIG), BIG)
+        return pl.ds(pl.multiple_of(block_of(k) * BIG, BIG), BIG)
 
     def x_load(k):
         return pltpu.make_async_copy(x_hbm.at[block_rows(k)], x_v.at[block_rows(k)], x_sem.at[k])
 
-    for k in range(n_sb):
-        x_load(k).start()
+    x_load(0).start()
     my_sg, my_tg = pos // n_tg, pos % n_tg
     y_load = pltpu.make_async_copy(y_hbm.at[pl.ds(pl.multiple_of(my_sg * TILE, TILE), TILE)], y_tile, in_sem.at[1])
-    y_load.start()
 
     def rs_copy(c, place, peer):
         return pltpu.make_async_remote_copy(src_ref=u_buf.at[c, place], dst_ref=rs_recv.at[c, pos], send_sem=rs_ssem.at[c],
@@ -78,13 +83,13 @@
                                             device_id_type=MESH)
 
     def keep_tiles(c, k, u):
-        sb = (my_sb + k + 1) % n_sb
+        sb = block_of(k)
         for j in range(per_sb):
             g, t = j // n_tg, j % n_tg
             u_buf[c, sb * per_sb + j] = u[t * th:(t + 1) * th, g * TILE:(g + 1) * TILE].astype(jnp.bfloat16)
 
     def send_tiles(c, k):
-        sb = (my_sb + k + 1) % n_sb
+        sb = block_of(k)
 
         def send(dz, dy, when):
             z, y = (mz + dz) % side, (my + dy) % side
@@ -128,12 +133,13 @@
     def gather_start(c):
         moves = [[moved(axis, by) for by in range(side)] for axis in axes(core % 3)]
         for a, b, d in far_first:
-            gather_copy(c, rb_full, pos, me + moves[0][a] + moves[1][b] + moves[2][d], ag_rsem.at[c]).start()
+            gather_copy(c, rb_full, pos, me + moves[0][a] + moves[1][b] + moves[2][d],
+                        ag_rsem.at[c, (a + b + d) % side]).start()
 
     def pass_on(c, place):
         ring = axes((c * n_samp + core) % 3)[0]
         for d in range(side - 1, 0, -1):
-            gather_copy(c, rf_full, place, me + moved(ring, d), ag_rsem.at[c]).start()
+            gather_copy(c, rf_full, place, me + moved(ring, d), ag_rsem.at[c, 0]).start()
 
     def last_gather_start(c):
         _, one, two = axes((c * n_samp + core) % 3)
@@ -149,14 +155,14 @@
             gather_copy(c, rf_full, place, me, ag_psem.at[c, i]).wait_recv()
             pass_on(c, place)
 
-    def gather_wait(c, ref, tiles):
+    def gather_wait(c, ref, tiles, q):
         part = ref.at[c, pl.ds(0, tiles)]
-        pltpu.make_async_remote_copy(src_ref=part, dst_ref=part, send_sem=ag_ssem.at[c], recv_sem=ag_rsem.at[c],
+        pltpu.make_async_remote_copy(src_ref=part, dst_ref=part, send_sem=ag_ssem.at[c], recv_sem=ag_rsem.at[c, q],
                                      device_id={"feat": me}, device_id_type=MESH).wait_recv()
 
     def gather_sent(c, ref):
         part = ref.at[c, pl.ds(1, n_feat - 1)]
-        pltpu.make_async_remote_copy(src_ref=part, dst_ref=part, send_sem=ag_ssem.at[c], recv_sem=ag_rsem.at[c],
+        pltpu.make_async_remote_copy(src_ref=part, dst_ref=part, send_sem=ag_ssem.at[c], recv_sem=ag_rsem.at[c, 0],
                                      device_id={"feat": me}, device_id_type=MESH).wait_send()
 
     def g_copy(c, par, f):
@@ -164,6 +170,9 @@
                                             recv_sem=g_rsem.at[par, c, f], device_id={"samp": 1 - core}, device_id_type=MESH)
 
     w_load.wait()
+    for k in range(1, n_sb):
+        x_load(k).start()
+    y_load.start()
     for f in range(n_fb):
         wt = w_nat[f * BIG:(f + 1) * BIG, :].T
         for c in range(CHAINS):
@@ -211,16 +220,16 @@
         rs_all(c).wait_send()
 
     def gradient_part(c, par):
-        gather_wait(c, rb_full, n_feat - 1)
-        rbt = jnp.concatenate([rb_full[c, g * n_tg:(g + 1) * n_tg].reshape(half, TILE) for g in range(n_sg)], axis=1)
-
-        def grad(f, _):
-            cols = pl.ds(pl.multiple_of(f * BIG, BIG), BIG)
-            gt[c, f] = jnp.dot(rbt, x_v[:, cols], preferred_element_type=jnp.float32)
-            g_copy(c, par, f).start()
-            return 0
-
-        lax.fori_loop(0, n_fb, grad, 0)
+        for n, q in enumerate(arrive):
+            gather_wait(c, rb_full, per_sb - (q == 0), q)
+            sb = (my_sb + side - q) % n_sb
+            block = pl.ds(pl.multiple_of(sb * BIG, BIG), BIG)
+            rbt = jnp.concatenate([rb_full[c, pl.ds(sb * per_sb + g * n_tg, n_tg)].reshape(half, TILE) for g in range(BIG // TILE)], axis=1)
+            for f in range(n_fb):
+                part = jnp.dot(rbt, x_v[block, f * BIG:(f + 1) * BIG], preferred_element_type=jnp.float32)
+                gt[c, f] = part if n == 0 else gt[c, f] + part
+                if n == len(arrive) - 1:
+                    g_copy(c, par, f).start()
 
     def step_and_product(c, par):
         lam = lam_t[c * half:(c + 1) * half, :]
@@ -270,7 +279,7 @@
         last_gather_forward(c)
 
     for c in range(CHAINS):
-        gather_wait(c, rf_full, n_feat - side * side)
+        gather_wait(c, rf_full, n_feat - side * side, 0)
     for g in range(n_sg):
         both = jnp.concatenate([rf_full[c, g * n_tg:(g + 1) * n_tg].reshape(half, TILE) for c in range(CHAINS)], axis=0)
         r_out[g * TILE:(g + 1) * TILE, :] = both.T
@@ -332,7 +341,7 @@
                 pltpu.SemaphoreType.DMA((CHAINS,)),
                 pltpu.SemaphoreType.DMA((CHAINS,)),
                 pltpu.SemaphoreType.DMA((CHAINS, side * side)),
-                pltpu.SemaphoreType.DMA((CHAINS,)),
+                pltpu.SemaphoreType.DMA((CHAINS, side)),
                 pltpu.SemaphoreType.DMA((CHAINS, n_fb)),
                 pltpu.SemaphoreType.DMA((2, CHAINS, n_fb)),
             ],

time: 111 us -> 112 us (level)
  no operation moved by 1% of the time
where the time goes in v8:
time: 112 us; the launch traced here: 111 us
  Pallas kernels  111 us (99%)
    pallas_call x1, Pallas kernels, local_sweeps(): pl.pallas_call(functools.partial(_kernel, side, n_feat, n_samp), name='de...  109 us

profile of v8, /device:TPU:0, one launch (start us, length us, event | category | flops | bytes accessed | tf_op | source)
XLA Modules:
  0.0 111.4 jit_solution(13139397542095274106)
XLA Ops:
  0.6 109.4 %descent.1 = (f32[2048,128]{1,0:T(8,128)S(1)}, f32[2048,128]{1,0:T(8,128)S(1)}) custom-call(bf16[2048,2048]{1,0:T(8,128)(2,1)} %x_hbm.1, f32[2048,128]{1,0:T(8,128)} %y_hbm.1, f32[2048,128]{1,0:T(8,128)} %w0_hbm.1, f32[1,2048]{1,0:T(1,128)} %bitcast.2, f32[1,128]{1,0:T(1,128)} %bitcast.3), custom_call_target="tpu_custom_call" | custom-call | tf_op jit(solution)/shard_map/descent/pallas_call | solution.py:317
  110.0 1.3 %write.1 = (f32[2048,128]{1,0:T(8,128)}, f32[2048,128]{1,0:T(8,128)}) custom-call(f32[2048,128]{1,0:T(8,128)S(1)} %get-tuple-element.4.w_ref, f32[2048,128]{1,0:T(8,128)S(1)} %get-tuple-element.5.r_ref), custom_call_target="tpu_custom_call" | custom-call | tf_op jit(solution)/shard_map/write/pallas_call | solution.py:350

commit v9 on v7

--- a/solution.py
+++ b/solution.py
@@ -34,6 +34,8 @@
     plane = sorted([(a, b) for a in steps for b in steps if a or b], key=lambda o: hops(*o))
     far_first = sorted([(a, b, d) for a in steps for b in steps for d in steps if a or b or d],
                        key=lambda o: (-hops(*o), (o[0] + 3 * o[1] + 5 * o[2]) % 7))
+    arrive = sorted(steps, key=lambda q: max(hops(*o) for o in far_first if sum(o) % side == q))
+    n_pair = 2 if side > 2 else 1
     per_sb = n_feat // n_sb
     total_rows = rows * n_samp
 
@@ -56,17 +58,21 @@
     my_sb, my_in_sb = (mx + my + mz) % side, mz * side + my
     pos = my_sb * per_sb + my_in_sb
 
+    def class_of(k):
+        return sum(jnp.where(k == i, q, 0) for i, q in enumerate(reversed(arrive)))
+
+    def block_of(k):
+        return (my_sb + class_of(k)) % n_sb
+
     def block_rows(k):
-        return pl.ds(pl.multiple_of(((my_sb + k + 1) % n_sb) * BIG, BIG), BIG)
+        return pl.ds(pl.multiple_of(block_of(k) * BIG, BIG), BIG)
 
     def x_load(k):
         return pltpu.make_async_copy(x_hbm.at[block_rows(k)], x_v.at[block_rows(k)], x_sem.at[k])
 
-    for k in range(n_sb):
-        x_load(k).start()
+    x_load(0).start()
     my_sg, my_tg = pos // n_tg, pos % n_tg
     y_load = pltpu.make_async_copy(y_hbm.at[pl.ds(pl.multiple_of(my_sg * TILE, TILE), TILE)], y_tile, in_sem.at[1])
-    y_load.start()
 
     def rs_copy(c, place, peer):
         return pltpu.make_async_remote_copy(src_ref=u_buf.at[c, place], dst_ref=rs_recv.at[c, pos], send_sem=rs_ssem.at[c],
@@ -78,13 +84,13 @@
                                             device_id_type=MESH)
 
     def keep_tiles(c, k, u):
-        sb = (my_sb + k + 1) % n_sb
+        sb = block_of(k)
         for j in range(per_sb):
             g, t = j // n_tg, j % n_tg
             u_buf[c, sb * per_sb + j] = u[t * th:(t + 1) * th, g * TILE:(g + 1) * TILE].astype(jnp.bfloat16)
 
     def send_tiles(c, k):
-        sb = (my_sb + k + 1) % n_sb
+        sb = block_of(k)
 
         def send(dz, dy, when):
             z, y = (mz + dz) % side, (my + dy) % side
@@ -125,10 +131,42 @@
         return pltpu.make_async_remote_copy(src_ref=ref.at[c, place], dst_ref=ref.at[c, place], send_sem=ag_ssem.at[c],
                                             recv_sem=recv_sem, device_id={"feat": peer}, device_id_type=MESH)
 
+    def first_stop(i):
+        def near(n):
+            return n + jnp.where(n == 2, 1, 0) - jnp.where(n == 3, 1, 0)
+
+        return lax.rem(i, n_pair) * (side - 1), near(lax.rem(lax.div(i, n_pair), side)), near(lax.div(i, n_pair * side))
+
+    def hop_on(c, place, i):
+        third = axes((c * n_samp + core) % 3)[0]
+        peer = me + jnp.where(lax.rem(i, n_pair) == 0, moved(third, 1), moved(third, side - 1))
+        gather_copy(c, rb_full, place, peer, ag_rsem.at[c]).start()
+
     def gather_start(c):
-        moves = [[moved(axis, by) for by in range(side)] for axis in axes(core % 3)]
-        for a, b, d in far_first:
-            gather_copy(c, rb_full, pos, me + moves[0][a] + moves[1][b] + moves[2][d], ag_rsem.at[c]).start()
+        (st0, at0), (st1, at1), (st2, at2) = axes((c * n_samp + core) % 3)
+
+        def send(n, _):
+            i = n_pair * side * side - 1 - n
+            r, a, b = first_stop(i)
+            peer = lax.rem(at0 + r, side) * st0 + lax.rem(at1 + a, side) * st1 + lax.rem(at2 + b, side) * st2
+            gather_copy(c, rb_full, pos, peer, ag_psem.at[c, i]).start()
+            return 0
+
+        lax.fori_loop(0, n_pair * side * side - 1, send, 0)
+        hop_on(c, pos, 0)
+
+    def gather_forward(c):
+        (st0, at0), (st1, at1), (st2, at2) = axes((c * n_samp + core) % 3)
+
+        def forward(i, _):
+            r, a, b = first_stop(i)
+            t, u, v = lax.rem(at0 + side - r, side), lax.rem(at1 + side - a, side), lax.rem(at2 + side - b, side)
+            place = lax.rem(t + u + v, side) * per_sb + lax.div(t * st0 + u * st1 + v * st2, side)
+            gather_copy(c, rb_full, place, me, ag_psem.at[c, i]).wait_recv()
+            hop_on(c, place, i)
+            return 0
+
+        lax.fori_loop(1, n_pair * side * side, forward, 0)
 
     def pass_on(c, place):
         ring = axes((c * n_samp + core) % 3)[0]
@@ -164,6 +202,9 @@
                                             recv_sem=g_rsem.at[par, c, f], device_id={"samp": 1 - core}, device_id_type=MESH)
 
     w_load.wait()
+    for k in range(1, n_sb):
+        x_load(k).start()
+    y_load.start()
     for f in range(n_fb):
         wt = w_nat[f * BIG:(f + 1) * BIG, :].T
         for c in range(CHAINS):
@@ -211,7 +252,7 @@
         rs_all(c).wait_send()
 
     def gradient_part(c, par):
-        gather_wait(c, rb_full, n_feat - 1)
+        gather_wait(c, rb_full, n_pair * side * side)
         rbt = jnp.concatenate([rb_full[c, g * n_tg:(g + 1) * n_tg].reshape(half, TILE) for g in range(n_sg)], axis=1)
 
         def grad(f, _):
@@ -250,20 +291,25 @@
 
     def sweep(s, last):
         par = s % 2
-        for c in range(CHAINS):
-            gradient_part(c, par)
-            step_and_product(c, par)
+        gradient_part(0, par)
+        gather_forward(1)
+        step_and_product(0, par)
+        gradient_part(1, par)
+        step_and_product(1, par)
         if last:
             for f in range(n_fb):
                 w_out[f * BIG:(f + 1) * BIG, :] = jnp.concatenate([w_t[c, f] for c in range(CHAINS)], axis=0).T
         for c in range(CHAINS):
             behind(c, STEP_WEIGHT, last)
+        if not last:
+            gather_forward(0)
 
     for c in range(CHAINS):
         rs_res[c] = y_tile[pl.ds(pl.multiple_of(c * half + my_tg * th, th), th), :]
     for c in range(CHAINS):
         behind(c, 1.0, False)
     lax.fori_loop(rows // MXU // 2, rows // MXU, turn, 0)
+    gather_forward(0)
     lax.fori_loop(0, SWEEPS - 1, lambda s, _: (sweep(s, False), 0)[1], 0)
     sweep(SWEEPS - 1, True)
     for c in range(CHAINS):
@@ -331,7 +377,7 @@
                 pltpu.SemaphoreType.DMA((CHAINS,)),
                 pltpu.SemaphoreType.DMA((CHAINS,)),
                 pltpu.SemaphoreType.DMA((CHAINS,)),
-                pltpu.SemaphoreType.DMA((CHAINS, side * side)),
+                pltpu.SemaphoreType.DMA((CHAINS, 2 * side * side)),
                 pltpu.SemaphoreType.DMA((CHAINS,)),
                 pltpu.SemaphoreType.DMA((CHAINS, n_fb)),
                 pltpu.SemaphoreType.DMA((2, CHAINS, n_fb)),

time: 111 us -> 125 us (1.13)
  Pallas kernels: 111 us -> 123 us
    pallas_call x1, Pallas kernels: 109 us -> 122 us  [local_sweeps(): pl.pallas_call(functools.partial(_kernel, side, n_feat, n_samp), name='de...]
where the time goes in v9:
time: 125 us; the launch traced here: 124 us
  Pallas kernels  123 us (98%)
    pallas_call x1, Pallas kernels, local_sweeps(): pl.pallas_call(functools.partial(_kernel, side, n_feat, n_samp), name='de...  122 us

profile of v9, /device:TPU:0, one launch (start us, length us, event | category | flops | bytes accessed | tf_op | source)
XLA Modules:
  0.0 124.1 jit_solution(5524413925088455027)
XLA Ops:
  0.6 122.1 %descent.1 = (f32[2048,128]{1,0:T(8,128)S(1)}, f32[2048,128]{1,0:T(8,128)S(1)}) custom-call(bf16[2048,2048]{1,0:T(8,128)(2,1)} %x_hbm.1, f32[2048,128]{1,0:T(8,128)} %y_hbm.1, f32[2048,128]{1,0:T(8,128)} %w0_hbm.1, f32[1,2048]{1,0:T(1,128)} %bitcast.2, f32[1,128]{1,0:T(1,128)} %bitcast.3), custom_call_target="tpu_custom_call" | custom-call | tf_op jit(solution)/shard_map/descent/pallas_call | solution.py:354
  122.8 1.3 %write.1 = (f32[2048,128]{1,0:T(8,128)}, f32[2048,128]{1,0:T(8,128)}) custom-call(f32[2048,128]{1,0:T(8,128)S(1)} %get-tuple-element.4.w_ref, f32[2048,128]{1,0:T(8,128)S(1)} %get-tuple-element.5.r_ref), custom_call_target="tpu_custom_call" | custom-call | tf_op jit(solution)/shard_map/write/pallas_call | solution.py:387

commit v10 on v8

--- a/solution.py
+++ b/solution.py
@@ -54,6 +54,7 @@
     w_load.start()
 
     mz, my, mx = me // (side * side), (me // side) % side, me % side
+    at_z, at_y = [lax.rem(mz + d, side) for d in steps], [lax.rem(my + d, side) for d in steps]
     my_sb, my_in_sb = (mx + my + mz) % side, mz * side + my
     pos = my_sb * per_sb + my_in_sb
 
@@ -61,7 +62,7 @@
         return sum(jnp.where(k == i, q, 0) for i, q in enumerate(reversed(arrive)))
 
     def block_of(k):
-        return (my_sb + class_of(k)) % n_sb
+        return lax.rem(my_sb + class_of(k), n_sb)
 
     def block_rows(k):
         return pl.ds(pl.multiple_of(block_of(k) * BIG, BIG), BIG)
@@ -92,9 +93,10 @@
         sb = block_of(k)
 
         def send(dz, dy, when):
-            z, y = (mz + dz) % side, (my + dy) % side
-            x = (sb + 2 * side - z - y) % side
-            copy = rs_copy(c, sb * per_sb + z * side + y, z * side * side + y * side + x)
+            z, y = at_z[dz], at_y[dy]
+            x = lax.rem(sb + 2 * side - z - y, side)
+            column = z * side + y
+            copy = rs_copy(c, sb * per_sb + column, column * side + x)
             if when is True:
                 copy.start()
             else:
@@ -261,6 +263,7 @@
         par = s % 2
         for c in range(CHAINS):
             gradient_part(c, par)
+        for c in range(CHAINS):
             step_and_product(c, par)
         if last:
             for f in range(n_fb):

time: 112 us -> 111 us (level)
  no operation moved by 1% of the time
where the time goes in v10:
time: 111 us
  Pallas kernels  110 us (99%)
    pallas_call x1, Pallas kernels, local_sweeps(): pl.pallas_call(functools.partial(_kernel, side, n_feat, n_samp), name='de...  109 us

profile of v10, /device:TPU:0, one launch (start us, length us, event | category | flops | bytes accessed | tf_op | source)
XLA Modules:
  0.0 110.7 jit_solution(11407823638297558607)
XLA Ops:
  0.6 108.7 %descent.1 = (f32[2048,128]{1,0:T(8,128)S(1)}, f32[2048,128]{1,0:T(8,128)S(1)}) custom-call(bf16[2048,2048]{1,0:T(8,128)(2,1)} %x_hbm.1, f32[2048,128]{1,0:T(8,128)} %y_hbm.1, f32[2048,128]{1,0:T(8,128)} %w0_hbm.1, f32[1,2048]{1,0:T(1,128)} %bitcast.2, f32[1,128]{1,0:T(1,128)} %bitcast.3), custom_call_target="tpu_custom_call" | custom-call | tf_op jit(solution)/shard_map/descent/pallas_call | solution.py:320
  109.3 1.3 %write.1 = (f32[2048,128]{1,0:T(8,128)}, f32[2048,128]{1,0:T(8,128)}) custom-call(f32[2048,128]{1,0:T(8,128)S(1)} %get-tuple-element.4.w_ref, f32[2048,128]{1,0:T(8,128)S(1)} %get-tuple-element.5.r_ref), custom_call_target="tpu_custom_call" | custom-call | tf_op jit(solution)/shard_map/write/pallas_call | solution.py:353

commit v11 on v10

--- a/solution.py
+++ b/solution.py
@@ -283,9 +283,8 @@
 
     for c in range(CHAINS):
         gather_wait(c, rf_full, n_feat - side * side, 0)
-    for g in range(n_sg):
-        both = jnp.concatenate([rf_full[c, g * n_tg:(g + 1) * n_tg].reshape(half, TILE) for c in range(CHAINS)], axis=0)
-        r_out[g * TILE:(g + 1) * TILE, :] = both.T
+        for g in range(n_sg):
+            r_out[g * TILE:(g + 1) * TILE, c * half:(c + 1) * half] = rf_full[c, g * n_tg:(g + 1) * n_tg].reshape(half, TILE).T
     for c in range(CHAINS):
         gather_sent(c, rf_full)
 

time: 111 us -> 112 us (level)
  no operation moved by 1% of the time
where the time goes in v11:
time: 112 us; the launch traced here: 111 us
  Pallas kernels  111 us (99%)
    pallas_call x1, Pallas kernels, local_sweeps(): pl.pallas_call(functools.partial(_kernel, side, n_feat, n_samp), name='de...  109 us

profile of v11, /device:TPU:0, one launch (start us, length us, event | category | flops | bytes accessed | tf_op | source)
XLA Modules:
  0.0 111.2 jit_solution(1277897537495279753)
XLA Ops:
  0.6 109.2 %descent.1 = (f32[2048,128]{1,0:T(8,128)S(1)}, f32[2048,128]{1,0:T(8,128)S(1)}) custom-call(bf16[2048,2048]{1,0:T(8,128)(2,1)} %x_hbm.1, f32[2048,128]{1,0:T(8,128)} %y_hbm.1, f32[2048,128]{1,0:T(8,128)} %w0_hbm.1, f32[1,2048]{1,0:T(1,128)} %bitcast.2, f32[1,128]{1,0:T(1,128)} %bitcast.3), custom_call_target="tpu_custom_call" | custom-call | tf_op jit(solution)/shard_map/descent/pallas_call | solution.py:319
  109.9 1.3 %write.1 = (f32[2048,128]{1,0:T(8,128)}, f32[2048,128]{1,0:T(8,128)}) custom-call(f32[2048,128]{1,0:T(8,128)S(1)} %get-tuple-element.4.w_ref, f32[2048,128]{1,0:T(8,128)S(1)} %get-tuple-element.5.r_ref), custom_call_target="tpu_custom_call" | custom-call | tf_op jit(solution)/shard_map/write/pallas_call | solution.py:352
